TPU v7x, 8 devices: a whole 2x2x1 slice. The times are simulated.
8 devices in a mesh: data: 8 (over z, y, x, core).
Axes of the slice: x: 2, y: 2, z: 1, core: 2. Of those that a mesh axis runs over, the one named last changes fastest.
Arguments:
- grad_attn: bfloat16 [8, 64, 16384], P('data')
- grad_mlp: bfloat16 [8, 32, 65536], P('data')
- grad_wide: bfloat16 [8, 16, 512], P('data')
- grad_vec: bfloat16 [8, 146, 128], P('data')
- weight_attn: float32 [64, 16384], P(None, 'data')
- weight_mlp: float32 [32, 65536], P(None, 'data')
- weight_wide: float32 [16, 512], P(None, 'data')
- weight_vec: float32 [146, 128], P(None, 'data')
- mom1_attn: float32 [64, 16384], P(None, 'data')
- mom1_mlp: float32 [32, 65536], P(None, 'data')
- mom1_wide: float32 [16, 512], P(None, 'data')
- mom1_vec: float32 [146, 128], P(None, 'data')
- mom2_attn: float32 [64, 16384], P(None, 'data')
- mom2_mlp: float32 [32, 65536], P(None, 'data')
- mom2_wide: float32 [16, 512], P(None, 'data')
- mom2_vec: float32 [146, 128], P(None, 'data')
Outputs:
- output 1: bfloat16 [64, 16384], replicated
- output 2: bfloat16 [32, 65536], replicated
- output 3: bfloat16 [16, 512], replicated
- output 4: bfloat16 [146, 128], replicated
- output 5: float32 [64, 16384], P(None, 'data')
- output 6: float32 [32, 65536], P(None, 'data')
- output 7: float32 [16, 512], P(None, 'data')
- output 8: float32 [146, 128], P(None, 'data')
- output 9: float32 [64, 16384], P(None, 'data')
- output 10: float32 [32, 65536], P(None, 'data')
- output 11: float32 [16, 512], P(None, 'data')
- output 12: float32 [146, 128], P(None, 'data')
- output 13: float32 [64, 16384], P(None, 'data')
- output 14: float32 [32, 65536], P(None, 'data')
- output 15: float32 [16, 512], P(None, 'data')
- output 16: float32 [146, 128], P(None, 'data')
All inputs are finite; a program needn't handle non-finite values.
Results may differ from a plain program's by a relative error of at most 0.001.
Values are sent between devices in bfloat16 or wider.
A program may use at most 1 GiB of HBM per device.

v0:
```python
import jax
import jax.numpy as jnp
from jax import lax
from jax.sharding import PartitionSpec as P

STEP_NUMBER = 10
LEARN_RATE = 0.04
BETA_FIRST = 0.9
BETA_SECOND = 0.999
EPSILON = 1e-6
WEIGHT_DECAY = 0.01
MAX_NORM = 1.0


def adam_direction(mean_grad, weight, first_moment, second_moment, clip_coef):
    clipped = clip_coef * mean_grad
    new_first = BETA_FIRST * first_moment + (1.0 - BETA_FIRST) * clipped
    new_second = BETA_SECOND * second_moment + (1.0 - BETA_SECOND) * (clipped * clipped)
    update = (new_first / (1.0 - BETA_FIRST ** STEP_NUMBER)) / (jnp.sqrt(new_second / (1.0 - BETA_SECOND ** STEP_NUMBER)) + EPSILON) + WEIGHT_DECAY * weight
    return update, new_first, new_second


def solution(mesh):
    group_size = mesh.shape["data"]
    grad_spec = P("data", None, None)
    shard_spec = P(None, "data")
    full_spec = P(None, None)

    def local_step(*all_banks):
        grad_banks = all_banks[0:4]
        weights = all_banks[4:8]
        firsts = all_banks[8:12]
        seconds = all_banks[12:16]
        mean_grads = []
        for grad_bank in grad_banks:
            row_count = grad_bank.shape[1]
            shard_width = grad_bank.shape[2] // group_size
            by_owner = grad_bank.reshape(row_count, group_size, shard_width)
            received = lax.all_to_all(by_owner, "data", 1, 1, tiled=True)
            mean_grads.append(jnp.sum(received, axis=1, dtype=jnp.float32) / group_size)
        local_square = sum(jnp.sum(mean_grad * mean_grad) for mean_grad in mean_grads)
        clip_coef = jnp.minimum(1.0, MAX_NORM / jnp.sqrt(lax.psum(local_square, "data")))
        results = [adam_direction(mean_grads[bank_index], weights[bank_index], firsts[bank_index], seconds[bank_index], clip_coef) for bank_index in range(4)]
        part_sums = jnp.concatenate([jnp.sum(weight * weight, axis=1) for weight in weights] + [jnp.sum(result[0] * result[0], axis=1) for result in results])
        norm_sums = lax.psum(part_sums, "data")
        tensor_count = norm_sums.shape[0] // 2
        trust_ratios = jnp.sqrt(norm_sums[:tensor_count]) / jnp.sqrt(norm_sums[tensor_count:])
        replicas, new_weights = [], []
        first_row = 0
        for bank_index in range(4):
            row_count = weights[bank_index].shape[0]
            trust_ratio = trust_ratios[first_row:first_row + row_count]
            first_row = first_row + row_count
            new_weight = weights[bank_index] - LEARN_RATE * trust_ratio[:, None] * results[bank_index][0]
            new_weights.append(new_weight)
            replicas.append(lax.all_gather(new_weight.astype(jnp.bfloat16), "data", axis=1, tiled=True))
        return tuple(replicas + new_weights + [result[1] for result in results] + [result[2] for result in results])

    return jax.shard_map(local_step, mesh=mesh, in_specs=(grad_spec,) * 4 + (shard_spec,) * 12, out_specs=(full_spec,) * 4 + (shard_spec,) * 12, check_vma=False)
```

profile of v0, /device:TPU:0, one launch (start us, length us, event | category | flops | bytes accessed | tf_op | source)
XLA Modules:
  0.0 237.3 jit_solution(9442735358529984781)
XLA Ops:
  8.7 4.3 %all-to-all-start.2 = ((bf16[8,2,512]{2,1,0:T(2,128)(2,1)}), bf16[8,2,512]{2,1,0:T(2,128)(2,1)S(1)}, u32[]{:S(2)}, u32[]{:S(2)}) async-start(bf16[8,2,512]{2,1,0:T(2,128)(2,1)} %reshape.58), calls=%async_computation.2 | async-start | bytes 32768 | tf_op jit(solution)/shard_map/all_to_all | solution.py:39
  13.0 1.5 copy.42
  14.5 3.0 %all-to-all-done.2 = bf16[8,2,512]{2,1,0:T(2,128)(2,1)S(1)} async-done(((bf16[8,2,512]{2,1,0:T(2,128)(2,1)}), bf16[8,2,512]{2,1,0:T(2,128)(2,1)S(1)}, u32[]{:S(2)}, u32[]{:S(2)}) %all-to-all-start.2) | async-done | bytes 16416 | tf_op jit(solution)/shard_map/all_to_all | solution.py:39
  17.6 2.1 all-to-all-start.3
  19.7 2.8 %copy.45 = bf16[8,8,8,2048]{3,2,1,0:T(8,128)(2,1)S(1)} copy(bf16[8,8,8,2048]{3,1,2,0:T(8,128)(2,1)} %bitcast.22) | data formatting | bytes 4194304
  22.4 2.5 %copy.39 = bf16[64,8,2048]{2,0,1:T(8,128)(2,1)} copy(bf16[64,8,2048]{2,1,0:T(8,128)(2,1)S(1)} %bitcast.20) | data formatting | bytes 4194304 | tf_op jit(solution)/shard_map/reshape | solution.py:38
  24.9 2.9 %all-to-all-start = ((bf16[64,8,2048]{2,0,1:T(8,128)(2,1)}), bf16[64,8,2048]{2,0,1:T(8,128)(2,1)S(1)}, u32[]{:S(2)}, u32[]{:S(2)}) async-start(bf16[64,8,2048]{2,0,1:T(8,128)(2,1)} %copy.39), calls=%async_computation | async-start | bytes 4194304 | tf_op jit(solution)/shard_map/all_to_all | solution.py:39
  27.8 4.5 %copy.46 = bf16[4,8,8,8192]{3,2,1,0:T(8,128)(2,1)S(1)} copy(bf16[4,8,8,8192]{3,1,2,0:T(8,128)(2,1)} %bitcast.21) | data formatting | bytes 8388608
  32.2 4.3 %copy.40 = bf16[32,8,8192]{2,0,1:T(8,128)(2,1)} copy(bf16[32,8,8192]{2,1,0:T(8,128)(2,1)S(1)} %bitcast.19) | data formatting | bytes 8388608 | tf_op jit(solution)/shard_map/reshape | solution.py:38
  36.6 17.8 %all-to-all-done = bf16[64,8,2048]{2,0,1:T(8,128)(2,1)S(1)} async-done(((bf16[64,8,2048]{2,0,1:T(8,128)(2,1)}), bf16[64,8,2048]{2,0,1:T(8,128)(2,1)S(1)}, u32[]{:S(2)}, u32[]{:S(2)}) %all-to-all-start) | async-done | bytes 2097184 | tf_op jit(solution)/shard_map/all_to_all | solution.py:39
  54.4 3.3 %all-to-all-start.1 = ((bf16[32,8,8192]{2,0,1:T(8,128)(2,1)}), bf16[32,8,8192]{2,0,1:T(8,128)(2,1)}, u32[]{:S(2)}, u32[]{:S(2)}) async-start(bf16[32,8,8192]{2,0,1:T(8,128)(2,1)} %copy.40), calls=%async_computation.1 | async-start | bytes 8388608 | tf_op jit(solution)/shard_map/all_to_all | solution.py:39
  60.1 46.5 %all-to-all-done.1 = bf16[32,8,8192]{2,0,1:T(8,128)(2,1)} async-done(((bf16[32,8,8192]{2,0,1:T(8,128)(2,1)}), bf16[32,8,8192]{2,0,1:T(8,128)(2,1)}, u32[]{:S(2)}, u32[]{:S(2)}) %all-to-all-start.1) | async-done | bytes 4194336 | tf_op jit(solution)/shard_map/all_to_all | solution.py:39
  106.6 2.9 %convert_reduce_fusion = f32[32,8192]{1,0:T(8,128)S(1)} fusion(bf16[32,8,8192]{2,0,1:T(8,128)(2,1)} %all-to-all-done.1), kind=kLoop, calls=%fused_computation | loop fusion | flops 3932160 | bytes 5242880 | tf_op jit(solution)/shard_map/reduce_sum | solution.py:40
  113.0 22.2 %psum.14 = f32[]{:T(128)} all-reduce(f32[]{:T(128)S(6)} %add.75), channel_id=1, replica_groups=mesh['data'=8] {'data'}, use_global_device_ids=true, to_apply=%region_12.0 | all-reduce | flops 1 | bytes 8 | tf_op jit(solution)/shard_map/psum | solution.py:42
  136.0 3.9 %multiply_reduce_fusion = (f32[32]{0:T(128)S(1)}, f32[32]{0:T(128)S(1)}, f32[32,8192]{1,0:T(8,128)}, f32[32,8192]{1,0:T(8,128)}) fusion(f32[32,8192]{1,0:T(8,128)S(1)} %copy-done.1, f32[32,8192]{1,0:T(8,128)S(1)} %convert_reduce_fusion, f32[]{:T(128)S(6)} %mul.261, f32[32,8192]{1,0:T(8,128)} %param.25, f32[32,8192]{1,0:T(8,128)} %param.29), kind=kLoop, calls=%fused_computation.3 | loop fusion | flops 4718528 | bytes 6291716 | tf_op jit(solution)/shard_map/reduce_sum | solution.py:44
  140.0 1.5 multiply_reduce_fusion.3
  141.9 23.4 %psum.15 = f32[516]{0:T(1024)S(1)} all-reduce(f32[516]{0:T(1024)S(1)} %concatenate.3), channel_id=1, replica_groups=mesh['data'=8] {'data'}, use_global_device_ids=true, to_apply=%region_17.0 | all-reduce | flops 516 | bytes 4128 | tf_op jit(solution)/shard_map/psum | solution.py:45
  165.4 2.4 %fusion.2 = (bf16[64,2048]{1,0:T(8,128)(2,1)}, f32[64,2048]{1,0:T(8,128)}) fusion(f32[64,2048]{1,0:T(8,128)S(1)} %copy-done.3, f32[64,2048]{1,0:T(8,128)} %get-tuple-element.132, f32[64,2048]{1,0:T(8,128)} %get-tuple-element.128, f32[64]{0:T(128)S(1)} %slice_multiply_fusion.3), kind=kLoop, calls=%fused_computation.40 | loop fusion | flops 1179648 | bytes 2359552 | tf_op jit(solution)/shard_map/convert_element_type | solution.py:56
  167.9 2.9 %fusion.1 = (bf16[32,8192]{1,0:T(8,128)(2,1)}, f32[32,8192]{1,0:T(8,128)}) fusion(f32[32,8192]{1,0:T(8,128)S(1)} %copy-done.1, f32[32,8192]{1,0:T(8,128)} %get-tuple-element.133, f32[32,8192]{1,0:T(8,128)S(1)} %copy-done.2, f32[32]{0:T(128)S(1)} %slice_multiply_fusion.2), kind=kLoop, calls=%fused_computation.39 | loop fusion | flops 2359296 | bytes 4718720 | tf_op jit(solution)/shard_map/convert_element_type | solution.py:56
  171.6 13.0 %all_gather.15 = bf16[146,128]{0,1:T(8,128)(2,1)S(1)} all-gather(bf16[146,16]{0,1:T(8,128)(2,1)S(1)} %get-tuple-element.88), channel_id=1, replica_groups=mesh['data'=8] {'data'}, dimensions={1}, use_global_device_ids=true | all-gather | bytes 42048 | tf_op jit(solution)/shard_map/all_gather | solution.py:56
  186.0 11.0 %all-gather = bf16[8,64,16]{1,2,0:T(8,128)(2,1)S(1)} all-gather(bf16[1,64,16]{1,2,0:T(8,128)(2,1)S(1)} %get-tuple-element.90), channel_id=1, replica_groups=mesh['data'=8] {'data'}, dimensions={0}, use_global_device_ids=true | all-gather | bytes 18432 | tf_op jit(solution)/shard_map/all_gather | solution.py:56
  197.7 27.5 %all-gather.6.cloned.1.call-done = bf16[32,65536]{1,0:T(8,128)(2,1)} async-done(((bf16[32,8192]{1,0:T(8,128)(2,1)}), bf16[32,65536]{1,0:T(8,128)(2,1)}) %all-gather.6.cloned.1.call-update) | async-done | bytes 4194320 | tf_op jit(solution)/shard_map/all_gather | solution.py:56
  225.3 3.2 %copy.51 = bf16[64,16384]{1,0:T(8,128)(2,1)} copy(bf16[64,16384]{1,0:T(8,128)(2,1)} %all-gather.4.cloned.1.call-done) | data formatting | bytes 4194304
  228.5 2.0 copy.52
  (62 shorter events, 8.3 us)
Async XLA Ops:
  8.7 8.8 %all-to-all-start.2 = ((bf16[8,2,512]{2,1,0:T(2,128)(2,1)}), bf16[8,2,512]{2,1,0:T(2,128)(2,1)S(1)}, u32[]{:S(2)}, u32[]{:S(2)}) async-start(bf16[8,2,512]{2,1,0:T(2,128)(2,1)} %reshape.58), calls=%async_computation.2 | async-start | bytes 32768 | tf_op jit(solution)/shard_map/all_to_all | solution.py:39
  17.6 7.3 %all-to-all-start.3 = ((bf16[146,8,16]{0,2,1:T(8,128)(2,1)}), bf16[146,8,16]{0,2,1:T(8,128)(2,1)S(1)}, u32[]{:S(2)}, u32[]{:S(2)}) async-start(bf16[146,8,16]{0,2,1:T(8,128)(2,1)} %bitcast), calls=%async_computation.3 | async-start | bytes 131072 | tf_op jit(solution)/shard_map/all_to_all | solution.py:39
  24.9 29.4 %all-to-all-start = ((bf16[64,8,2048]{2,0,1:T(8,128)(2,1)}), bf16[64,8,2048]{2,0,1:T(8,128)(2,1)S(1)}, u32[]{:S(2)}, u32[]{:S(2)}) async-start(bf16[64,8,2048]{2,0,1:T(8,128)(2,1)} %copy.39), calls=%async_computation | async-start | bytes 4194304 | tf_op jit(solution)/shard_map/all_to_all | solution.py:39
  54.4 52.3 %all-to-all-start.1 = ((bf16[32,8,8192]{2,0,1:T(8,128)(2,1)}), bf16[32,8,8192]{2,0,1:T(8,128)(2,1)}, u32[]{:S(2)}, u32[]{:S(2)}) async-start(bf16[32,8,8192]{2,0,1:T(8,128)(2,1)} %copy.40), calls=%async_computation.1 | async-start | bytes 8388608 | tf_op jit(solution)/shard_map/all_to_all | solution.py:39
  57.6 140.1 %all-gather.4.cloned.1.call-start = ((), (), s32[]{:S(2)}) async-start(), calls=%async_computation.4 | async-start | bytes 2359296 | tf_op jit(solution)/shard_map/all_gather | solution.py:56
  59.4 76.6 %copy-start.1 = (f32[32,8192]{1,0:T(8,128)S(1)}, f32[32,8192]{1,0:T(8,128)}, u32[]{:S(2)}) copy-start(f32[32,8192]{1,0:T(8,128)} %param.21) | copy-start | bytes 3145732
  109.5 30.4 %copy-start.3 = (f32[64,2048]{1,0:T(8,128)S(1)}, f32[64,2048]{1,0:T(8,128)}, u32[]{:S(2)}) copy-start(f32[64,2048]{1,0:T(8,128)} %param.20) | copy-start | bytes 1572868
  136.0 4.0 %copy-start.4 = (f32[64,2048]{1,0:T(8,128)S(1)}, f32[64,2048]{1,0:T(8,128)}, u32[]{:S(2)}) copy-start(f32[64,2048]{1,0:T(8,128)} %param.24) | copy-start | bytes 1572868
  136.0 4.0 %copy-start.5 = (f32[64,2048]{1,0:T(8,128)S(1)}, f32[64,2048]{1,0:T(8,128)}, u32[]{:S(2)}) copy-start(f32[64,2048]{1,0:T(8,128)} %param.28) | copy-start | bytes 1572868
  136.0 5.5 %copy-start.9 = (f32[16,64]{1,0:T(8,128)S(1)}, f32[16,64]{1,0:T(8,128)}, u32[]{:S(2)}) copy-start(f32[16,64]{1,0:T(8,128)} %param.22) | copy-start | bytes 12292
  136.0 5.5 %copy-start.14 = (f32[16,64]{1,0:T(8,128)S(1)}, f32[16,64]{1,0:T(8,128)}, u32[]{:S(2)}) copy-start(f32[16,64]{1,0:T(8,128)} %param.26) | copy-start | bytes 12292
  136.0 5.5 %copy-start.15 = (f32[16,64]{1,0:T(8,128)S(1)}, f32[16,64]{1,0:T(8,128)}, u32[]{:S(2)}) copy-start(f32[16,64]{1,0:T(8,128)} %param.30) | copy-start | bytes 12292
  136.0 5.7 %copy-start.6 = (f32[146,16]{0,1:T(8,128)S(1)}, f32[146,16]{0,1:T(8,128)}, u32[]{:S(2)}) copy-start(f32[146,16]{0,1:T(8,128)} %param.23) | copy-start | bytes 28036
  136.0 5.6 %copy-start.12 = (f32[146,16]{0,1:T(8,128)S(1)}, f32[146,16]{0,1:T(8,128)}, u32[]{:S(2)}) copy-start(f32[146,16]{0,1:T(8,128)} %param.27) | copy-start | bytes 28036
  136.0 5.6 %copy-start.13 = (f32[146,16]{0,1:T(8,128)S(1)}, f32[146,16]{0,1:T(8,128)}, u32[]{:S(2)}) copy-start(f32[146,16]{0,1:T(8,128)} %param.31) | copy-start | bytes 28036
  140.0 27.9 %copy-start.2 = (f32[32,8192]{1,0:T(8,128)S(1)}, f32[32,8192]{1,0:T(8,128)}, u32[]{:S(2)}) copy-start(f32[32,8192]{1,0:T(8,128)} %get-tuple-element.129) | copy-start | bytes 3145732
  141.7 55.3 %copy-start.10 = (f32[16,64]{1,0:T(8,128)}, f32[16,64]{1,0:T(8,128)S(1)}, u32[]{:S(2)}) copy-start(f32[16,64]{1,0:T(8,128)S(1)} %get-tuple-element.130) | copy-start | bytes 12292
  141.7 55.3 %copy-start.11 = (f32[16,64]{1,0:T(8,128)}, f32[16,64]{1,0:T(8,128)S(1)}, u32[]{:S(2)}) copy-start(f32[16,64]{1,0:T(8,128)S(1)} %get-tuple-element.134) | copy-start | bytes 12292
  141.8 83.5 %copy-start.7 = (f32[146,16]{0,1:T(8,128)}, f32[146,16]{0,1:T(8,128)S(1)}, u32[]{:S(2)}) copy-start(f32[146,16]{0,1:T(8,128)S(1)} %get-tuple-element.131) | copy-start | bytes 28036
  141.8 83.5 %copy-start.8 = (f32[146,16]{0,1:T(8,128)}, f32[146,16]{0,1:T(8,128)S(1)}, u32[]{:S(2)}) copy-start(f32[146,16]{0,1:T(8,128)S(1)} %get-tuple-element.135) | copy-start | bytes 28036
  167.8 57.5 %all-gather.6.cloned.1.call-start = ((), (), s32[]{:S(2)}) async-start(), calls=%async_computation.5 | async-start | bytes 4718592 | tf_op jit(solution)/shard_map/all_gather | solution.py:56
  225.3 3.2 %copy-start = (bf16[32,65536]{1,0:T(8,128)(2,1)S(1)}, bf16[32,65536]{1,0:T(8,128)(2,1)}, u32[]{:S(2)}) copy-start(bf16[32,65536]{1,0:T(8,128)(2,1)} %all-gather.6.cloned.1.call-done) | copy-start | bytes 12582916
Sparse Core Ops, SparseCore 0:
  167.9 24.1 all-gather.3
  194.5 30.7 all-gather.5
where the time goes:
time: 238 us; the launch traced here: 237 us
  waiting for transfers between devices  94.9 us (40%)
  blocking collectives  69.6 us (29%)
  local copies, waits for them, and re-layouts  24 us (10%)
  other arithmetic  18.6 us (8%)
  between operations  17.6 us (7%)
  starting transfers between devices  12.6 us (5%)
    all_to_all x4, waiting for transfers between devices, local_step(): received = lax.all_to_all(by_owner, 'data', 1, 1, tiled=True)  67.3 us
    all_gather x2, waiting for transfers between devices, local_step(): lax.all_gather(new_weight.astype(jnp.bfloat16), 'data', axis=1, tiled=True)  27.5 us
    all_gather x2, blocking collectives, local_step(): lax.all_gather(new_weight.astype(jnp.bfloat16), 'data', axis=1, tiled=True)  23.9 us
    psum x1, blocking collectives, local_step(): norm_sums = lax.psum(part_sums, 'data')  23.4 us
    psum x1, blocking collectives, local_step(): lax.psum(local_square, 'data')  22.2 us
    unnamed x41, local copies, waits for them, and re-layouts  16.3 us
    all_to_all x4, starting transfers between devices, local_step(): received = lax.all_to_all(by_owner, 'data', 1, 1, tiled=True)  12.5 us
    reshape x4, local copies, waits for them, and re-layouts, local_step(): by_owner = grad_bank.reshape(row_count, group_size, shard_width)  7.6 us
  transfers between devices with their start and end apart: 6, of which 4 were waited for; matrix products, arithmetic and copies ran while one was open for 10% of the time, Pallas kernels for 0%

commit v1 on v0

v1 whole, which is shorter than its diff:
```python
import functools

import jax
import jax.numpy as jnp
from jax import lax
from jax.experimental import pallas as pl
from jax.experimental.pallas import tpu as pltpu
from jax.sharding import PartitionSpec as P

STEP_NUMBER = 10
LEARN_RATE = 0.04
BETA_FIRST = 0.9
BETA_SECOND = 0.999
EPSILON = 1e-6
WEIGHT_DECAY = 0.01
MAX_NORM = 1.0
FIRST_SCALE = 1.0 / (1.0 - BETA_FIRST ** STEP_NUMBER)
SECOND_SCALE = 1.0 / (1.0 - BETA_SECOND ** STEP_NUMBER)

MESH = pl.DeviceIdType.MESH
LANES = 128
TALL = 16
VEC = 146
VEC_PAD = 256
ATTN_SHARD = 2048
MLP_SHARD = 8192
PIECE = 4096
STEP = 1024
BLOCK = 512
CHUNKS = 3
MIB = 2 ** 20
PEERS = range(1, 8)
CHUNK_HALVES = tuple((chunk, half) for chunk in range(CHUNKS) for half in range(2))
ROWS = (64, 32, TALL, VEC)
LENGTHS = (16384, 65536, BLOCK, LANES)
SHARDS = ((64, ATTN_SHARD), (32, MLP_SHARD), (TALL, 64), (TALL, VEC))


def flip(index, mask):
    core, x, y = index % 2, (index // 2) % 2, index // 4
    if mask & 1:
        core = 1 - core
    if mask & 2:
        x = 1 - x
    if mask & 4:
        y = 1 - y
    return y * 4 + x * 2 + core


def direction(first, weight, second, total, clip):
    clipped = clip * total
    new_first = BETA_FIRST * first + (1.0 - BETA_FIRST) * clipped
    new_second = BETA_SECOND * second + (1.0 - BETA_SECOND) * (clipped * clipped)
    update = (new_first * FIRST_SCALE) / (jnp.sqrt(new_second * SECOND_SCALE) + EPSILON) + WEIGHT_DECAY * weight
    return update, new_first, new_second


def fold(square):
    rows, columns = square.shape
    parts = [square[r:r + 8, k:k + LANES] for r in range(0, rows, 8) for k in range(0, columns, LANES)]
    while len(parts) > 1:
        parts = [a + b for a, b in zip(parts[::2], parts[1::2])] + ([parts[-1]] if len(parts) % 2 else [])
    return parts[0]


def kernel(*refs):
    grads, weights, firsts, seconds = refs[0:4], refs[4:8], refs[8:12], refs[12:TALL]
    replicas, new_weights, new_firsts, new_seconds = refs[TALL:20], refs[20:24], refs[24:28], refs[28:32]
    (recv_attn, recv_mlp, part_attn, part_mlp, last_attn, last_mlp, sum_attn, sum_mlp, sum_wide, sum_vec,
     recv_wide, recv_vec, vec_out, vec_in, vec_wide, vec_tall, vec_wide2, all_wide, all_vec,
     norm_tiles, weight_tiles, update_tiles, rows_acc, vec_row,
     scatter_recv, scatter_send, state_sem, last_send, last_recv, wide_send, wide_recv, vec_send, vec_recv,
     tile_send, tile_recv, own_send, own_recv, pass_send, pass_recv, pair_send, pair_recv,
     small_send, small_recv) = refs[32:]
    me = lax.axis_index("data")
    core = me % 2
    near = ((2, 4), (4, 2))

    loads = []
    for source, target in ((weights, new_weights), (firsts, new_firsts), (seconds, new_seconds)):
        for bank in range(4):
            loads.append(pltpu.make_async_copy(source[bank], target[bank], state_sem.at[len(loads)]))

    def grad_chunk(half, owner, chunk):
        if chunk < 2:
            start = pl.multiple_of(owner * MLP_SHARD + chunk * PIECE, PIECE)
            return grads[1].at[pl.ds(TALL * half, TALL), pl.ds(start, PIECE)]
        return grads[0].at[pl.ds(32 * half, 32), pl.ds(pl.multiple_of(owner * ATTN_SHARD, ATTN_SHARD), ATTN_SHARD)]

    def recv_chunk(half, keep, slot, chunk):
        if chunk < 2:
            return recv_mlp.at[half, keep, slot, :, pl.ds(chunk * PIECE, PIECE)]
        return recv_attn.at[half, keep, slot]

    def pair_chunk(attn, mlp, half, chunk):
        if chunk < 2:
            return mlp.at[half, :, pl.ds(chunk * PIECE, PIECE)]
        return attn.at[half]

    def replica_chunk(half, owner, chunk):
        if chunk < 2:
            start = pl.multiple_of(owner * MLP_SHARD + chunk * PIECE, PIECE)
            return replicas[1].at[pl.ds(TALL * half, TALL), pl.ds(start, PIECE)]
        return replicas[0].at[pl.ds(32 * half, 32), pl.ds(pl.multiple_of(owner * ATTN_SHARD, ATTN_SHARD), ATTN_SHARD)]

    def remote(source, target, send, recv, device):
        return pltpu.make_async_remote_copy(src_ref=source, dst_ref=target, send_sem=send, recv_sem=recv,
                                            device_id=(device,), device_id_type=MESH)

    own = {}
    for keep in range(2):
        for chunk in range(CHUNKS):
            for half in range(2):
                owner = me if keep else flip(me, near[half][1])
                own[half, keep, chunk] = pltpu.make_async_copy(
                    grad_chunk(half, owner, chunk), recv_chunk(half, keep, 0, chunk), scatter_recv.at[half, keep, 0, chunk])
                own[half, keep, chunk].start()
    for load in loads:
        load.start()
    wide_own = pltpu.make_async_copy(
        grads[2].at[:, pl.ds(pl.multiple_of((me // 2) * LANES, LANES), LANES)], recv_wide.at[me], wide_recv.at[0])
    wide_own.start()
    vec_load = pltpu.make_async_copy(grads[3], vec_in, vec_recv.at[0])
    vec_load.start()

    barrier = pltpu.get_barrier_semaphore()
    for mask in PEERS:
        pl.semaphore_signal(barrier, inc=1, device_id=(flip(me, mask),), device_id_type=MESH)
    pl.semaphore_wait(barrier, 7)

    sends = []

    def send(*copy):
        copy = remote(*copy)
        copy.start()
        sends.append(copy)
        return copy

    def scatter(keep):
        for chunk in range(CHUNKS):
            for slot in range(3):
                for half in range(2):
                    target = flip(me, 1) if slot == 0 else flip(me, near[half][0]) // 2 * 2 + slot - 1
                    owner = target if keep else flip(target, near[half][1])
                    index = 1 if slot == 0 else 2 + core
                    send(grad_chunk(half, owner, chunk), recv_chunk(half, keep, index, chunk),
                         scatter_send.at[half, keep, slot, chunk], scatter_recv.at[half, keep, index, chunk], target)

    scatter(0)

    vec_load.wait()
    vec_wide[...] = jnp.zeros_like(vec_wide)
    vec_wide[0:VEC, :] = vec_in[...].astype(jnp.float32)
    vec_out[...] = vec_wide[...].T.astype(jnp.bfloat16)
    recv_vec[me] = vec_out[pl.ds(pl.multiple_of(me * TALL, TALL), TALL), :]
    small = []
    for mask in PEERS:
        target = flip(me, mask)
        small.append(send(grads[2].at[:, pl.ds(pl.multiple_of((target // 2) * LANES, LANES), LANES)], recv_wide.at[me],
                          wide_send.at[mask], wide_recv.at[mask], target))
        small.append(send(vec_out.at[pl.ds(pl.multiple_of(target * TALL, TALL), TALL), :], recv_vec.at[me],
                          vec_send.at[mask], vec_recv.at[mask], target))
    scatter(1)

    def exchange(tiles, which, value):
        tiles[me] = value
        return [send(tiles.at[me], tiles.at[me], tile_send.at[which, mask], tile_recv.at[which, mask], flip(me, mask))
                for mask in PEERS]

    def collect(tiles, copies):
        for copy in copies:
            copy.wait_recv()
        total = tiles[0]
        for index in PEERS:
            total = total + tiles[index]
        return total

    row = lax.broadcasted_iota(jnp.int32, (LANES, LANES), 0)
    lane = lax.broadcasted_iota(jnp.int32, (LANES, LANES), 1)
    eye = row == lane
    sub = lax.broadcasted_iota(jnp.int32, (8, LANES), 0)

    def norm_tile(acc, vec_square):
        column = jnp.sum(acc[...], axis=1, keepdims=True)
        lanes = jnp.sum(jnp.where(eye, column, 0.0), axis=0, keepdims=True)
        vec_row[...] = jnp.zeros_like(vec_row)
        vec_row[0:1, 0:VEC] = jnp.sum(vec_square, axis=0, keepdims=True)
        low, high = vec_row[0:1, 0:LANES], vec_row[0:1, LANES:VEC_PAD]
        return jnp.where(sub == 0, lanes, jnp.where(sub == 1, low, jnp.where(sub == 2, high, 0.0)))

    for load in loads:
        load.wait()
    rows_acc[...] = jnp.zeros_like(rows_acc)

    def square_rows(ref, first, groups, columns):
        def group(g, carry):
            rows = pl.ds(pl.multiple_of(g * 8, 8), 8)

            def step(j, acc):
                value = ref[rows, pl.ds(pl.multiple_of(j * STEP, STEP), STEP)]
                return acc + fold(value * value)

            rows_acc[pl.ds(pl.multiple_of(first + g * 8, 8), 8), :] = lax.fori_loop(
                0, columns // STEP, step, jnp.zeros((8, LANES), jnp.float32))
            return carry

        lax.fori_loop(0, groups, group, 0)

    square_rows(new_weights[0], 0, 8, ATTN_SHARD)
    square_rows(new_weights[1], 64, 4, MLP_SHARD)
    wide_weight, vec_weight = new_weights[2][...], new_weights[3][...]
    rows_acc[96:112, 0:64] = wide_weight * wide_weight
    weight_copies = exchange(weight_tiles, 0, norm_tile(rows_acc, vec_weight * vec_weight))

    wide_own.wait()
    for copy in small:
        copy.wait_recv()
    wide_total = recv_wide[0].astype(jnp.float32)
    vec_total = recv_vec[0].astype(jnp.float32)
    for index in PEERS:
        wide_total = wide_total + recv_wide[index].astype(jnp.float32)
        vec_total = vec_total + recv_vec[index].astype(jnp.float32)
    wide_total = jnp.where(core == 0, wide_total[:, 0:64], wide_total[:, 64:LANES])
    sum_wide[...] = wide_total
    vec_total = vec_total[:, 0:VEC]
    sum_vec[...] = vec_total

    def blocks(chunk, step, init):
        rows, columns = (TALL, PIECE) if chunk < 2 else (32, ATTN_SHARD)
        for r in range(0, rows, TALL):
            init = lax.fori_loop(0, columns // BLOCK, functools.partial(
                lambda first, j, carry: step(first, pl.multiple_of(j * BLOCK, BLOCK), carry), r), init)
        return init

    def gather_sum(half, keep, chunk):
        own[half, keep, chunk].wait()
        for slot in range(1, 4):
            remote(recv_chunk(half, keep, slot, chunk), recv_chunk(half, keep, slot, chunk),
                   scatter_send.at[half, keep, 0, chunk], scatter_recv.at[half, keep, slot, chunk], flip(me, 1)).wait_recv()

        def step(r, c, carry):
            if chunk < 2:
                value = [recv_mlp[half, keep, s, :, pl.ds(chunk * PIECE + c, BLOCK)].astype(jnp.float32) for s in range(4)]
            else:
                value = [recv_attn[half, keep, s, r:r + TALL, pl.ds(c, BLOCK)].astype(jnp.float32) for s in range(4)]
            value = (value[0] + value[1]) + (value[2] + value[3])
            if keep:
                if chunk < 2:
                    sum_mlp[TALL * half:TALL * half + TALL, pl.ds(chunk * PIECE + c, BLOCK)] = value
                else:
                    sum_attn[32 * half + r:32 * half + r + TALL, pl.ds(c, BLOCK)] = value
            elif chunk < 2:
                part_mlp[half, :, pl.ds(chunk * PIECE + c, BLOCK)] = value
            else:
                part_attn[half, r:r + TALL, pl.ds(c, BLOCK)] = value
            return carry

        blocks(chunk, step, 0)

    last = {}
    for chunk, half in CHUNK_HALVES:
        gather_sum(half, 0, chunk)
        last[half, chunk] = send(
            pair_chunk(part_attn, part_mlp, half, chunk), pair_chunk(last_attn, last_mlp, half, chunk),
            last_send.at[half, chunk], last_recv.at[half, chunk], flip(me, near[half][1]))
    for chunk, half in CHUNK_HALVES:
        gather_sum(half, 1, chunk)

    square = jnp.concatenate([wide_total * wide_total, jnp.zeros((TALL, 64), jnp.float32)], axis=1)
    square = fold(square)
    vec_row[...] = jnp.zeros_like(vec_row)
    vec_row[0:1, 0:VEC] = jnp.sum(vec_total * vec_total, axis=0, keepdims=True)
    square = square + vec_row[:, 0:LANES] + vec_row[:, LANES:VEC_PAD]
    for chunk, half in CHUNK_HALVES:
        last[half, chunk].wait_recv()

        def step(r, c, acc):
            if chunk < 2:
                place = (slice(TALL * half, TALL * half + TALL), pl.ds(chunk * PIECE + c, BLOCK))
                value = sum_mlp[place] + last_mlp[half, :, pl.ds(chunk * PIECE + c, BLOCK)]
                sum_mlp[place] = value
            else:
                place = (slice(32 * half + r, 32 * half + r + TALL), pl.ds(c, BLOCK))
                value = sum_attn[place] + last_attn[half, r:r + TALL, pl.ds(c, BLOCK)]
                sum_attn[place] = value
            return acc + fold(value * value)

        square = blocks(chunk, step, square)

    square = collect(norm_tiles, exchange(norm_tiles, 1, square))
    square = jnp.sum(jnp.sum(square, axis=1, keepdims=True), axis=0, keepdims=True)
    clip = jnp.minimum(1.0, (8.0 * MAX_NORM) / jnp.sqrt(jnp.broadcast_to(square, (8, LANES)))) * 0.125

    rows_acc[...] = jnp.zeros_like(rows_acc)
    clip_block = jnp.concatenate([clip] * 8, axis=1)

    def update_rows(bank, totals, first, groups, columns):
        def group(g, carry):
            rows = pl.ds(pl.multiple_of(g * 8, 8), 8)

            def step(j, acc):
                place = (rows, pl.ds(pl.multiple_of(j * STEP, STEP), STEP))
                update, new_first, new_second = direction(
                    new_firsts[bank][place], new_weights[bank][place], new_seconds[bank][place], totals[place], clip_block)
                totals[place] = update
                new_firsts[bank][place] = new_first
                new_seconds[bank][place] = new_second
                return acc + fold(update * update)

            rows_acc[pl.ds(pl.multiple_of(first + g * 8, 8), 8), :] = lax.fori_loop(
                0, columns // STEP, step, jnp.zeros((8, LANES), jnp.float32))
            return carry

        lax.fori_loop(0, groups, group, 0)

    update_rows(0, sum_attn, 0, 8, ATTN_SHARD)
    update_rows(1, sum_mlp, 64, 4, MLP_SHARD)
    wide_update, new_first, new_second = direction(
        new_firsts[2][...], wide_weight, new_seconds[2][...], sum_wide[...], clip[0:1, 0:1])
    new_firsts[2][...] = new_first
    new_seconds[2][...] = new_second
    rows_acc[96:112, 0:64] = wide_update * wide_update
    vec_update, new_first, new_second = direction(
        new_firsts[3][...], vec_weight, new_seconds[3][...], sum_vec[...], clip[0:1, 0:1])
    new_firsts[3][...] = new_first
    new_seconds[3][...] = new_second
    update_copies = exchange(update_tiles, 2, norm_tile(rows_acc, vec_update * vec_update))
    weight_norms = jnp.sqrt(collect(weight_tiles, weight_copies))
    ratio = LEARN_RATE * (weight_norms / jnp.sqrt(collect(update_tiles, update_copies)))
    rows_acc[...] = jnp.broadcast_to(
        jnp.sum(jnp.where(eye, ratio[0:1, :], 0.0), axis=1, keepdims=True), (LANES, LANES))

    own_copies = {}

    def send_own(half, chunk, way):
        device = flip(me, (1, 2, 4)[way])
        place = replica_chunk(half, me, chunk)
        own_copies[half, chunk, way] = send(
            place, place, own_send.at[half, chunk, way], own_recv.at[half, chunk, way], device)

    for chunk, half in CHUNK_HALVES:
        def step(r, c, carry):
            bank = 1 if chunk < 2 else 0
            first = TALL * half if chunk < 2 else 32 * half + r
            column = chunk * PIECE + c if chunk < 2 else c
            scale = jnp.concatenate([rows_acc[64 * bank + first:64 * bank + first + TALL, :]] * (BLOCK // LANES), axis=1)
            place = (slice(first, first + TALL), pl.ds(column, BLOCK))
            totals = sum_mlp if bank else sum_attn
            value = new_weights[bank][place] - scale * totals[place]
            new_weights[bank][place] = value
            start = pl.multiple_of(me * SHARDS[bank][1] + column, BLOCK)
            replicas[bank][first:first + TALL, pl.ds(start, BLOCK)] = value.astype(jnp.bfloat16)
            return carry

        blocks(chunk, step, 0)
        send_own(half, chunk, 1 + half)
        send_own(half, chunk, 0)
    for chunk, half in CHUNK_HALVES:
        send_own(half, chunk, 2 - half)

    value = wide_weight - rows_acc[96:112, 0:64] * wide_update
    new_weights[2][...] = value
    all_wide[me] = jnp.concatenate([value, value], axis=1).astype(jnp.bfloat16)
    vec_row[0:1, 0:LANES] = ratio[1:2, :]
    vec_row[0:1, LANES:VEC_PAD] = ratio[2:3, :]
    value = vec_weight - vec_row[0:1, 0:VEC] * vec_update
    new_weights[3][...] = value
    vec_wide2[...] = jnp.zeros_like(vec_wide2)
    vec_wide2[:, 0:VEC] = value
    all_vec[me] = vec_wide2[...].astype(jnp.bfloat16)
    small = []
    for mask in PEERS:
        target = flip(me, mask)
        small.append(send(all_wide.at[me], all_wide.at[me], small_send.at[0, mask], small_recv.at[0, mask], target))
        small.append(send(all_vec.at[me], all_vec.at[me], small_send.at[1, mask], small_recv.at[1, mask], target))

    pair = []

    def send_pair(half, owner, chunk, slot):
        place = replica_chunk(half, owner, chunk)
        pair.append(send(place, place, pair_send.at[half, chunk, slot], pair_recv.at[half, chunk, slot], flip(me, 1)))

    passed = {}
    for chunk, half in CHUNK_HALVES:
        own_copies[half, chunk, 1 + half].wait_recv()
        owner = flip(me, near[half][0])
        place = replica_chunk(half, owner, chunk)
        passed[half, chunk] = send(place, place, pass_send.at[half, chunk], pass_recv.at[half, chunk],
                                   flip(me, near[half][1]))
        send_pair(half, owner, chunk, 0)
    for copy in small:
        copy.wait_recv()
    low_lanes = lax.broadcasted_iota(jnp.int32, (TALL, LANES), 1) < 64
    for index in range(4):
        tile = jnp.where(low_lanes, all_wide[2 * index].astype(jnp.float32), all_wide[2 * index + 1].astype(jnp.float32))
        replicas[2][:, LANES * index:LANES * index + LANES] = tile.astype(jnp.bfloat16)
    for index in range(8):
        vec_tall[TALL * index:TALL * index + TALL, :] = all_vec[index].astype(jnp.float32)
    vec_wide[...] = vec_tall[...].T
    replicas[3][...] = vec_wide[0:VEC, :].astype(jnp.bfloat16)
    for chunk, half in CHUNK_HALVES:
        own_copies[half, chunk, 2 - half].wait_recv()
        send_pair(half, flip(me, near[half][1]), chunk, 1)
    for chunk, half in CHUNK_HALVES:
        passed[half, chunk].wait_recv()
        send_pair(half, flip(me, 6), chunk, 2)
    for chunk, half in CHUNK_HALVES:
        own_copies[half, chunk, 0].wait_recv()
    for copy in pair:
        copy.wait_recv()
    for copy in sends:
        copy.wait_send()


def write_out(*refs):
    count = (len(refs) - 1) // 2
    copies = [pltpu.make_async_copy(refs[k], refs[count + k], refs[-1].at[k]) for k in range(count)]
    for copy in copies:
        copy.start()
    for copy in copies:
        copy.wait()


def solution(mesh):
    shards = [jax.ShapeDtypeStruct(shape, jnp.float32) for shape in SHARDS]
    shapes = [jax.ShapeDtypeStruct(shape, jnp.bfloat16) for shape in zip(ROWS, LENGTHS)] + shards * 3
    f32, bf16, vmem = jnp.float32, jnp.bfloat16, pltpu.VMEM
    dma = pltpu.SemaphoreType.DMA
    scratch = [
        vmem((2, 2, 4, 32, ATTN_SHARD), bf16), vmem((2, 2, 4, TALL, MLP_SHARD), bf16),
        vmem((2, 32, ATTN_SHARD), f32), vmem((2, TALL, MLP_SHARD), f32), vmem((2, 32, ATTN_SHARD), f32), vmem((2, TALL, MLP_SHARD), f32),
        vmem((64, ATTN_SHARD), f32), vmem((32, MLP_SHARD), f32), vmem((TALL, 64), f32), vmem((TALL, VEC), f32),
        vmem((8, TALL, LANES), bf16), vmem((8, TALL, VEC_PAD), bf16), vmem((LANES, VEC_PAD), bf16),
        vmem((VEC, LANES), bf16), vmem((VEC_PAD, LANES), f32), vmem((LANES, VEC_PAD), f32), vmem((TALL, VEC_PAD), f32),
        vmem((8, TALL, LANES), bf16), vmem((8, TALL, VEC_PAD), bf16),
        vmem((8, 8, LANES), f32), vmem((8, 8, LANES), f32), vmem((8, 8, LANES), f32), vmem((LANES, LANES), f32), vmem((8, VEC_PAD), f32),
        dma((2, 2, 4, CHUNKS)), dma((2, 2, 3, CHUNKS)), dma((12,)), dma((2, CHUNKS)), dma((2, CHUNKS)),
        dma((8,)), dma((8,)), dma((8,)), dma((8,)), dma((3, 8)), dma((3, 8)),
        dma((2, CHUNKS, 3)), dma((2, CHUNKS, 3)), dma((2, CHUNKS)), dma((2, CHUNKS)),
        dma((2, CHUNKS, 3)), dma((2, CHUNKS, 3)), dma((2, 8)), dma((2, 8)),
    ]
    step = pl.pallas_call(
        kernel,
        out_shape=[pltpu.VMEM(shape.shape, shape.dtype) for shape in shapes],
        in_specs=[pl.BlockSpec(memory_space=pl.ANY)] * TALL,
        out_specs=[pl.BlockSpec(memory_space=pltpu.VMEM)] * TALL,
        scratch_shapes=scratch,
        compiler_params=pltpu.CompilerParams(collective_id=0, has_side_effects=True, vmem_limit_bytes=36 * MIB),
        name="lamb_step",
    )
    finish = pl.pallas_call(
        write_out,
        out_shape=shapes,
        in_specs=[pl.BlockSpec(memory_space=pl.ANY)] * TALL,
        out_specs=[pl.BlockSpec(memory_space=pl.ANY)] * TALL,
        scratch_shapes=[dma((TALL,))],
        compiler_params=pltpu.CompilerParams(vmem_limit_bytes=MIB),
        name="write_out",
    )

    def local_step(*banks):
        banks = [bank[0] for bank in banks[:4]] + [bank.T if bank.shape == (VEC, TALL) else bank for bank in banks[4:]]
        banks = [pltpu.with_memory_space_constraint(bank, pltpu.HBM) for bank in banks]
        results = finish(*step(*banks))
        return tuple(value.T if value.shape == (TALL, VEC) else value for value in results)

    grad_spec, shard_spec, full_spec = P("data", None, None), P(None, "data"), P(None, None)
    return jax.shard_map(local_step, mesh=mesh, in_specs=(grad_spec,) * 4 + (shard_spec,) * 12,
                         out_specs=(full_spec,) * 4 + (shard_spec,) * 12, check_vma=False)
```

time: 238 us -> 105 us (0.44)
  Pallas kernels: 0 us -> 104 us
  waiting for transfers between devices: 94.9 us -> 0 us
  blocking collectives: 69.6 us -> 0 us
  local copies, waits for them, and re-layouts: 24 us -> 0 us
  other arithmetic: 18.6 us -> 0 us
  between operations: 17.6 us -> 0.66 us
  starting transfers between devices: 12.6 us -> 0 us
    pallas_call x0 -> x2, Pallas kernels: none -> 104 us  [local_step(): results = finish(*step(*banks))]
    all_to_all x4 -> x0, waiting for transfers between devices: 67.3 us -> none  [local_step(): received = lax.all_to_all(by_owner, 'data', 1, 1, tiled=True)]
    psum x2 -> x0, blocking collectives: 45.7 us -> none  [the longest x1 23.4 us: local_step(): norm_sums = lax.psum(part_sums, 'data')]
    all_gather x2 -> x0, waiting for transfers between devices: 27.5 us -> none  [local_step(): lax.all_gather(new_weight.astype(jnp.bfloat16), 'data', axis=1, tiled=True)]
    all_gather x2 -> x0, blocking collectives: 23.9 us -> none  [local_step(): lax.all_gather(new_weight.astype(jnp.bfloat16), 'data', axis=1, tiled=True)]
    unnamed x41 -> x0, local copies, waits for them, and re-layouts: 16.3 us -> none
    all_to_all x4 -> x0, starting transfers between devices: 12.5 us -> none  [local_step(): received = lax.all_to_all(by_owner, 'data', 1, 1, tiled=True)]
    reduce_sum x12 -> x0, other arithmetic: 11.7 us -> none  [the longest x4 5.59 us: local_step(): jnp.sum(result[0] * result[0], axis=1)]
  transfers between devices with their start and end apart: 6 -> 0, of which waited for: 4 -> 0; matrix products, arithmetic and copies ran while one was open for 10% -> 0% of each run, Pallas kernels for 0% -> 0%
where the time goes in v1:
time: 105 us
  Pallas kernels  104 us (99%)
    pallas_call x2, Pallas kernels, local_step(): results = finish(*step(*banks))  104 us

profile of v1, /device:TPU:0, one launch (start us, length us, event | category | flops | bytes accessed | tf_op | source)
XLA Modules:
  0.0 104.7 jit_solution(10356735580920581902)
XLA Ops:
  0.7 99.7 %lamb_step.1 = (bf16[64,16384]{1,0:T(8,128)(2,1)S(1)}, bf16[32,65536]{1,0:T(8,128)(2,1)S(1)}, bf16[16,512]{1,0:T(8,128)(2,1)S(1)}, bf16[146,128]{1,0:T(8,128)(2,...) custom-call(bf16[64,16384]{1,0:T(8,128)(2,1)} %bitcast.11, ...), custom_call_target="tpu_custom_call" | custom-call | tf_op jit(solution)/shard_map/lamb_step/pallas_call | solution.py:464
  100.3 4.3 %write_out.1 = (bf16[64,16384]{1,0:T(8,128)(2,1)}, bf16[32,65536]{1,0:T(8,128)(2,1)}, bf16[16,512]{1,0:T(8,128)(2,1)}, bf16[146,128]{1,0:T(8,128)(2,1)}, f32[64,...) custom-call(bf16[64,16384]{1,0:T(8,128)(2,1)S(1)} %get-tuple-element, ...), custom_call_target="tpu_custom_call" | custom-call | tf_op jit(solution)/shard_map/write_out/pallas_call | solution.py:464

commit v2 on v0

v2 whole, which is shorter than its diff:
```python
import functools

import jax
import jax.numpy as jnp
from jax import lax
from jax.experimental import pallas as pl
from jax.experimental.pallas import tpu as pltpu
from jax.sharding import PartitionSpec as P

STEP_NUMBER = 10
LEARN_RATE = 0.04
BETA_FIRST = 0.9
BETA_SECOND = 0.999
EPSILON = 1e-6
WEIGHT_DECAY = 0.01
MAX_NORM = 1.0
FIRST_SCALE = 1.0 / (1.0 - BETA_FIRST ** STEP_NUMBER)
SECOND_SCALE = 1.0 / (1.0 - BETA_SECOND ** STEP_NUMBER)

MESH = pl.DeviceIdType.MESH
LANES = 128
TALL = 16
HALF = 64
VEC = 146
VEC_PAD = 256
ATTN_SHARD = 2048
MLP_SHARD = 8192
STEP = 1024
BLOCK = 512
MIB = 2 ** 20
ROWS = (HALF, 32, TALL, VEC)
LENGTHS = (16384, 65536, BLOCK, LANES)
SHARDS = ((HALF, ATTN_SHARD), (32, MLP_SHARD), (TALL, HALF), (TALL, VEC))
ATTN, MLP, SMALL = range(3)
HALVES = range(2)
SHAPES = ((32, ATTN_SHARD), (TALL, MLP_SHARD))
PEER, ALONG_X, ALONG_Y = 1, 2, 4
NEAR = ((ALONG_X, ALONG_Y), (ALONG_Y, ALONG_X))
FAR_FIRST = tuple(reversed(range(1, 8)))


def flip(index, mask):
    core, x, y = index % 2, (index // 2) % 2, index // 4
    if mask & PEER:
        core = 1 - core
    if mask & ALONG_X:
        x = 1 - x
    if mask & ALONG_Y:
        y = 1 - y
    return y * 4 + x * 2 + core


def aligned(index, size):
    return pl.ds(pl.multiple_of(index * size, size), size)


def moments(first, second, total, clip):
    clipped = clip * total
    new_first = BETA_FIRST * first + (1.0 - BETA_FIRST) * clipped
    new_second = BETA_SECOND * second + (1.0 - BETA_SECOND) * (clipped * clipped)
    return new_first, new_second


def direction(new_first, new_second, weight):
    return (new_first * FIRST_SCALE) / (jnp.sqrt(new_second * SECOND_SCALE) + EPSILON) + WEIGHT_DECAY * weight


def fold(square):
    rows, columns = square.shape
    parts = [square[r:r + 8, k:k + LANES] for r in range(0, rows, 8) for k in range(0, columns, LANES)]
    while len(parts) > 1:
        parts = [a + b for a, b in zip(parts[::2], parts[1::2])] + ([parts[-1]] if len(parts) % 2 else [])
    return parts[0]


def add_all(values):
    return functools.reduce(lambda a, b: a + b, values)


def kernel(*refs):
    grads, weights, firsts, seconds = refs[0:4], refs[4:8], refs[8:12], refs[12:16]
    replicas, new_weights, new_firsts, new_seconds = refs[16:20], refs[20:24], refs[24:28], refs[28:32]
    (recv_attn, recv_mlp, recv_wide, recv_vec, part_attn, part_mlp, part_wide, part_vec,
     last_attn, last_mlp, last_wide, last_vec, sum_attn, sum_mlp, sum_wide, sum_vec, dir_attn, dir_mlp,
     vec_in, vec_out, vec_rows, vec_columns, vec_row, all_wide, all_vec, start_tiles, attn_tiles, rest_tiles, row_acc,
     state_sem, vec_sem, scatter_send, scatter_recv, last_send, last_recv, tile_send, tile_recv,
     own_send, own_recv, pass_send, pass_recv, pair_send, pair_recv) = refs[32:]
    me = lax.axis_index("data")
    core = me % 2

    def grad_chunk(half, owner, chunk):
        if chunk == MLP:
            return grads[1].at[pl.ds(TALL * half, TALL), aligned(owner, MLP_SHARD)]
        if chunk == ATTN:
            return grads[0].at[pl.ds(32 * half, 32), aligned(owner, ATTN_SHARD)]
        return vec_out.at[aligned(owner, TALL), :] if half else grads[2].at[:, aligned(owner // 2, LANES)]

    def recv_chunk(half, keep, slot, chunk):
        if chunk == SMALL:
            return (recv_vec if half else recv_wide).at[keep, slot]
        return (recv_attn, recv_mlp)[chunk].at[half, keep, slot]

    def sum_chunk(half, chunk, buffers):
        if chunk == SMALL:
            return buffers[3] if half else buffers[2]
        return buffers[chunk].at[half]

    parts, lasts = (part_attn, part_mlp, part_wide, part_vec), (last_attn, last_mlp, last_wide, last_vec)

    def replica_chunk(half, owner, chunk):
        if chunk == MLP:
            return replicas[1].at[pl.ds(TALL * half, TALL), aligned(owner, MLP_SHARD)]
        if chunk == ATTN:
            return replicas[0].at[pl.ds(32 * half, 32), aligned(owner, ATTN_SHARD)]
        return (all_vec if half else all_wide).at[owner]

    def remote(source, target, send_sem, recv_sem, device):
        return pltpu.make_async_remote_copy(src_ref=source, dst_ref=target, send_sem=send_sem, recv_sem=recv_sem,
                                            device_id=(device,), device_id_type=MESH)

    sends = []

    def send(*copy):
        copy = remote(*copy)
        copy.start()
        sends.append(copy)
        return copy

    vec_load = pltpu.make_async_copy(grads[3], vec_in, vec_sem)
    vec_load.start()
    own = {}
    for keep in range(2):
        for half in HALVES:
            for chunk in (MLP, ATTN, SMALL)[:3 - half]:
                owner = me if keep else flip(me, NEAR[half][1])
                own[half, keep, chunk] = pltpu.make_async_copy(
                    grad_chunk(half, owner, chunk), recv_chunk(half, keep, 0, chunk), scatter_recv.at[half, keep, 0, chunk])
                own[half, keep, chunk].start()
    loads = []
    for source, target in ((weights, new_weights), (firsts, new_firsts), (seconds, new_seconds)):
        for bank in range(4):
            loads.append(pltpu.make_async_copy(source[bank], target[bank], state_sem.at[len(loads)]))
            loads[-1].start()

    barrier = pltpu.get_barrier_semaphore()
    near = (1, 2, 3, 4, 5)
    for mask in near:
        pl.semaphore_signal(barrier, inc=1, device_id=(flip(me, mask),), device_id_type=MESH)
    pl.semaphore_wait(barrier, len(near))

    def scatter(keep, chunk):
        for slot in range(3):
            for half in HALVES:
                target = flip(me, PEER) if slot == 0 else flip(me, NEAR[half][0]) // 2 * 2 + slot - 1
                owner = target if keep else flip(target, NEAR[half][1])
                index = 1 if slot == 0 else 2 + core
                send(grad_chunk(half, owner, chunk), recv_chunk(half, keep, index, chunk),
                     scatter_send.at[half, keep, slot, chunk], scatter_recv.at[half, keep, index, chunk], target)

    scatter(0, MLP)
    scatter(0, ATTN)
    vec_load.wait()
    vec_rows[...] = jnp.zeros_like(vec_rows)
    vec_rows[0:VEC, :] = vec_in[...].astype(jnp.float32)
    vec_out[...] = vec_rows[...].T.astype(jnp.bfloat16)
    recv_vec[0, 0] = vec_out[aligned(flip(me, NEAR[1][1]), TALL), :]
    recv_vec[1, 0] = vec_out[aligned(me, TALL), :]
    scatter(0, SMALL)
    scatter(1, MLP)
    scatter(1, ATTN)
    scatter(1, SMALL)

    row = lax.broadcasted_iota(jnp.int32, (LANES, LANES), 0)
    lane = lax.broadcasted_iota(jnp.int32, (LANES, LANES), 1)
    eye = row == lane
    sub = lax.broadcasted_iota(jnp.int32, (8, LANES), 0)

    def lanes_of(first, last):
        column = jnp.sum(row_acc[first:last, :], axis=1, keepdims=True)
        return jnp.sum(jnp.where(eye[first:last, :], column, 0.0), axis=0, keepdims=True)

    def vec_lanes(square):
        vec_row[...] = jnp.zeros_like(vec_row)
        vec_row[0:1, 0:VEC] = jnp.sum(square, axis=0, keepdims=True)
        return vec_row[0:1, 0:LANES], vec_row[0:1, LANES:VEC_PAD]

    def tile_of(rows):
        tile = jnp.zeros((8, LANES), jnp.float32)
        for index, value in enumerate(rows):
            tile = jnp.where(sub == index, value, tile)
        return tile

    def exchange(tiles, which, value):
        tiles[me] = value
        return [send(tiles.at[me], tiles.at[me], tile_send.at[which, mask], tile_recv.at[which, mask], flip(me, mask))
                for mask in FAR_FIRST]

    def collect(tiles, copies):
        for copy in copies:
            copy.wait_recv()
        return add_all([tiles[index] for index in range(8)])

    def by_rows(first, groups, columns, step):
        def group(g, carry):
            def inner(j, acc):
                return acc + step((aligned(g, 8), aligned(j, STEP)))

            row_acc[pl.ds(pl.multiple_of(first + g * 8, 8), 8), :] = lax.fori_loop(
                0, columns // STEP, inner, jnp.zeros((8, LANES), jnp.float32))
            return carry

        lax.fori_loop(0, groups, group, 0)

    def square_of(ref):
        return lambda place: fold(ref[place] * ref[place])

    for load in loads:
        load.wait()
    row_acc[...] = jnp.zeros_like(row_acc)
    by_rows(0, 8, ATTN_SHARD, square_of(new_weights[0]))
    by_rows(HALF, 4, MLP_SHARD, square_of(new_weights[1]))
    wide_weight, vec_weight = new_weights[2][...], new_weights[3][...]
    row_acc[96:112, 0:HALF] = wide_weight * wide_weight
    weight_lanes = lanes_of(0, LANES)
    weight_low, weight_high = vec_lanes(vec_weight * vec_weight)

    def by_blocks(chunk, step, init):
        rows, columns = SHAPES[chunk]
        for r in range(0, rows, TALL):
            init = lax.fori_loop(0, columns // BLOCK, functools.partial(
                lambda first, j, carry: step((pl.ds(first, TALL), aligned(j, BLOCK)), carry), r), init)
        return init

    def gather_sum(half, keep, chunk):
        if (half, keep, chunk) in own:
            own[half, keep, chunk].wait()
        for slot in range(1, 4):
            place = recv_chunk(half, keep, slot, chunk)
            remote(place, place, scatter_send.at[half, keep, 0, chunk], scatter_recv.at[half, keep, slot, chunk],
                   flip(me, PEER)).wait_recv()
        target = sum_chunk(half, chunk, (sum_attn, sum_mlp, sum_wide, sum_vec) if keep else parts)
        sources = [recv_chunk(half, keep, slot, chunk) for slot in range(4)]
        if chunk == SMALL:
            target[...] = add_all([source[...].astype(jnp.float32) for source in sources])
            return

        def step(place, carry):
            value = [source[place].astype(jnp.float32) for source in sources]
            target[place] = (value[0] + value[1]) + (value[2] + value[3])
            return carry

        by_blocks(chunk, step, 0)

    last = {}
    for chunk in (MLP, ATTN, SMALL):
        for half in HALVES:
            gather_sum(half, 0, chunk)
    for chunk in (SMALL, MLP, ATTN):
        for half in HALVES:
            last[half, chunk] = send(
                sum_chunk(half, chunk, parts), sum_chunk(half, chunk, lasts),
                last_send.at[half, chunk], last_recv.at[half, chunk], flip(me, NEAR[half][1]))
    for chunk in (MLP, ATTN, SMALL):
        for half in HALVES:
            gather_sum(half, 1, chunk)

    for half in HALVES:
        last[half, SMALL].wait_recv()
    wide_total = sum_wide[...] + last_wide[...]
    wide_total = jnp.where(core == 0, wide_total[:, 0:HALF], wide_total[:, HALF:LANES])
    vec_total = (sum_vec[...] + last_vec[...])[:, 0:VEC]
    square = fold(jnp.concatenate([wide_total * wide_total, jnp.zeros((TALL, HALF), jnp.float32)], axis=1))
    low, high = vec_lanes(vec_total * vec_total)
    square = square + tile_of([low, high])
    for chunk in (MLP, ATTN):
        for half in HALVES:
            last[half, chunk].wait_recv()
            total, rest = sum_chunk(half, chunk, (sum_attn, sum_mlp)), sum_chunk(half, chunk, lasts)

            def step(place, acc):
                value = total[place] + rest[place]
                total[place] = value
                return acc + fold(value * value)

            square = by_blocks(chunk, step, square)

    start = collect(start_tiles, exchange(start_tiles, 0, tile_of(
        [weight_lanes, weight_low, weight_high, jnp.sum(square, axis=0, keepdims=True)])))
    square = jnp.sum(jnp.sum(start[3:4, :], axis=1, keepdims=True), axis=0, keepdims=True)
    clip = jnp.minimum(1.0, (8.0 * MAX_NORM) / jnp.sqrt(jnp.broadcast_to(square, (8, LANES)))) * 0.125
    clip_block = jnp.concatenate([clip] * (STEP // LANES), axis=1)
    weight_norms = LEARN_RATE * jnp.sqrt(start)

    sums, directions = (sum_attn, sum_mlp), (dir_attn, dir_mlp)

    def update(bank, half):
        rows = SHAPES[bank][0]

        def step(place):
            state = (pl.ds(pl.multiple_of(half * rows + place[0].start, 8), 8), place[1])
            new_first, new_second = moments(
                new_firsts[bank][state], new_seconds[bank][state], sums[bank].at[half][place], clip_block)
            value = direction(new_first, new_second, new_weights[bank][state])
            directions[bank].at[half][place] = value
            return fold(value * value)

        by_rows(HALF * bank + half * rows, rows // 8, SHAPES[bank][1], step)

    def store_moments(bank, half):
        rows = SHAPES[bank][0]

        def step(place, carry):
            state = (pl.ds(half * rows + place[0].start, TALL), place[1])
            clip_wide = jnp.concatenate([clip_block[:, 0:BLOCK]] * 2, axis=0)
            new_first, new_second = moments(
                new_firsts[bank][state], new_seconds[bank][state], sums[bank].at[half][place], clip_wide)
            new_firsts[bank][state] = new_first
            new_seconds[bank][state] = new_second
            return carry

        by_blocks(bank, step, 0)

    def update_small(bank, total, weight):
        new_first, new_second = moments(new_firsts[bank][...], new_seconds[bank][...], total, clip[0:1, 0:1])
        new_firsts[bank][...] = new_first
        new_seconds[bank][...] = new_second
        return direction(new_first, new_second, weight)

    for half in HALVES:
        update(ATTN, half)
    attn_copies = exchange(attn_tiles, 1, tile_of([lanes_of(0, HALF)]))
    for half in HALVES:
        update(MLP, half)
    wide_dir = update_small(2, wide_total, wide_weight)
    vec_dir = update_small(3, vec_total, vec_weight)
    row_acc[96:112, 0:HALF] = wide_dir * wide_dir
    rest_copies = exchange(rest_tiles, 2, tile_of([lanes_of(HALF, LANES), *vec_lanes(vec_dir * vec_dir)]))
    for bank in (ATTN, MLP):
        for half in HALVES:
            store_moments(bank, half)

    own_copies = {}

    def send_own(half, chunk, way):
        place = replica_chunk(half, me, chunk)
        own_copies[half, chunk, way] = send(place, place, own_send.at[half, chunk, way], own_recv.at[half, chunk, way],
                                            flip(me, (PEER, ALONG_X, ALONG_Y)[way]))

    def spread_ratio(first, last, ratio):
        row_acc[first:last, :] = jnp.broadcast_to(
            jnp.sum(jnp.where(eye[first:last, :], ratio[0:1, :], 0.0), axis=1, keepdims=True), (last - first, LANES))

    def new_weight(bank, half):
        rows, columns = SHAPES[bank]

        def step(place, carry):
            first = half * rows + place[0].start
            scale = jnp.concatenate([row_acc[HALF * bank + first:HALF * bank + first + TALL, :]] * (BLOCK // LANES), axis=1)
            state = (pl.ds(first, TALL), place[1])
            value = new_weights[bank][state] - scale * directions[bank].at[half][place]
            new_weights[bank][state] = value
            target = pl.ds(pl.multiple_of(me * columns + place[1].start, BLOCK), BLOCK)
            replicas[bank][pl.ds(first, TALL), target] = value.astype(jnp.bfloat16)
            return carry

        by_blocks(bank, step, 0)
        send_own(half, bank, 1 + half)
        send_own(half, bank, 0)

    spread_ratio(0, HALF, weight_norms / jnp.sqrt(collect(attn_tiles, attn_copies)))
    for half in HALVES:
        new_weight(ATTN, half)
    ratio = weight_norms / jnp.sqrt(collect(rest_tiles, rest_copies))
    spread_ratio(HALF, LANES, ratio)
    for half in HALVES:
        new_weight(MLP, half)
    value = wide_weight - row_acc[96:112, 0:HALF] * wide_dir
    new_weights[2][...] = value
    all_wide[me] = jnp.concatenate([value, value], axis=1).astype(jnp.bfloat16)
    vec_row[0:1, 0:LANES] = ratio[1:2, :]
    vec_row[0:1, LANES:VEC_PAD] = ratio[2:3, :]
    value = vec_weight - vec_row[0:1, 0:VEC] * vec_dir
    new_weights[3][...] = value
    vec_columns[0:TALL, :] = jnp.zeros((TALL, VEC_PAD), jnp.float32)
    vec_columns[0:TALL, 0:VEC] = value
    all_vec[me] = vec_columns[0:TALL, :].astype(jnp.bfloat16)
    for half in HALVES:
        send_own(half, SMALL, 1 + half)
        send_own(half, SMALL, 0)
    for chunk in (ATTN, MLP, SMALL):
        for half in HALVES:
            send_own(half, chunk, 2 - half)

    pairs = {}

    def send_pair(half, owner, chunk, slot):
        place = replica_chunk(half, owner, chunk)
        pairs[half, chunk, slot] = send(
            place, place, pair_send.at[half, chunk, slot], pair_recv.at[half, chunk, slot], flip(me, PEER))

    passed = {}
    for chunk in (SMALL, MLP, ATTN):
        for half in HALVES:
            own_copies[half, chunk, 1 + half].wait_recv()
            owner = flip(me, NEAR[half][0])
            place = replica_chunk(half, owner, chunk)
            passed[half, chunk] = send(place, place, pass_send.at[half, chunk], pass_recv.at[half, chunk],
                                       flip(me, NEAR[half][1]))
            send_pair(half, owner, chunk, 0)
    for chunk in (ATTN, MLP, SMALL):
        for half in HALVES:
            own_copies[half, chunk, 2 - half].wait_recv()
            send_pair(half, flip(me, NEAR[half][1]), chunk, 1)
    for chunk in (SMALL, MLP, ATTN):
        for half in HALVES:
            passed[half, chunk].wait_recv()
            send_pair(half, flip(me, ALONG_X + ALONG_Y), chunk, 2)
            if chunk == SMALL:
                own_copies[half, chunk, 0].wait_recv()
                for slot in range(3):
                    pairs[half, chunk, slot].wait_recv()
        if chunk == SMALL:
            low_lanes = lax.broadcasted_iota(jnp.int32, (TALL, LANES), 1) < HALF
            for index in range(4):
                left, right = (all_wide[2 * index + k].astype(jnp.float32) for k in range(2))
                replicas[2][:, pl.ds(LANES * index, LANES)] = jnp.where(low_lanes, left, right).astype(jnp.bfloat16)
            for index in range(8):
                vec_columns[pl.ds(TALL * index, TALL), :] = all_vec[index].astype(jnp.float32)
            vec_rows[...] = vec_columns[...].T
            replicas[3][...] = vec_rows[0:VEC, :].astype(jnp.bfloat16)
    for chunk in (ATTN, MLP):
        for half in HALVES:
            own_copies[half, chunk, 0].wait_recv()
            for slot in range(3):
                pairs[half, chunk, slot].wait_recv()
    for copy in sends:
        copy.wait_send()


def write_out(*refs):
    count = (len(refs) - 1) // 2
    copies = [pltpu.make_async_copy(refs[k], refs[count + k], refs[-1].at[k]) for k in range(count)]
    for copy in copies:
        copy.start()
    for copy in copies:
        copy.wait()


def solution(mesh):
    shards = [jax.ShapeDtypeStruct(shape, jnp.float32) for shape in SHARDS]
    shapes = [jax.ShapeDtypeStruct(shape, jnp.bfloat16) for shape in zip(ROWS, LENGTHS)] + shards * 3
    f32, bf16 = jnp.float32, jnp.bfloat16
    dma = pltpu.SemaphoreType.DMA
    attn, mlp = SHAPES

    def sums(*lead):
        return [pltpu.VMEM((*lead, *attn), f32), pltpu.VMEM((*lead, *mlp), f32)]

    small_sums = [pltpu.VMEM((TALL, LANES), f32), pltpu.VMEM((TALL, VEC_PAD), f32)]
    scratch = [
        pltpu.VMEM((2, 2, 4, *attn), bf16), pltpu.VMEM((2, 2, 4, *mlp), bf16),
        pltpu.VMEM((2, 4, TALL, LANES), bf16), pltpu.VMEM((2, 4, TALL, VEC_PAD), bf16),
        *sums(2), *small_sums, *sums(2), *small_sums, *sums(2), *small_sums, *sums(2),
        pltpu.VMEM((VEC, LANES), bf16), pltpu.VMEM((LANES, VEC_PAD), bf16),
        pltpu.VMEM((VEC_PAD, LANES), f32), pltpu.VMEM((LANES, VEC_PAD), f32), pltpu.VMEM((8, VEC_PAD), f32),
        pltpu.VMEM((8, TALL, LANES), bf16), pltpu.VMEM((8, TALL, VEC_PAD), bf16),
        *[pltpu.VMEM((8, 8, LANES), f32)] * 3, pltpu.VMEM((LANES, LANES), f32),
        dma((12,)), dma, dma((2, 2, 3, 3)), dma((2, 2, 4, 3)), dma((2, 3)), dma((2, 3)), dma((3, 8)), dma((3, 8)),
        dma((2, 3, 3)), dma((2, 3, 3)), dma((2, 3)), dma((2, 3)), dma((2, 3, 3)), dma((2, 3, 3)),
    ]
    count = len(shapes)
    anywhere = [pl.BlockSpec(memory_space=pl.ANY)] * count
    step = pl.pallas_call(
        kernel,
        out_shape=[pltpu.VMEM(shape.shape, shape.dtype) for shape in shapes],
        in_specs=anywhere,
        out_specs=[pl.BlockSpec(memory_space=pltpu.VMEM)] * count,
        scratch_shapes=scratch,
        compiler_params=pltpu.CompilerParams(collective_id=0, has_side_effects=True, vmem_limit_bytes=36 * MIB),
        name="lamb_step",
    )
    finish = pl.pallas_call(
        write_out,
        out_shape=shapes,
        in_specs=anywhere,
        out_specs=anywhere,
        scratch_shapes=[dma((count,))],
        compiler_params=pltpu.CompilerParams(vmem_limit_bytes=MIB),
        name="write_out",
    )

    def local_step(*banks):
        banks = [bank[0] for bank in banks[:4]] + [bank.T if bank.shape == (VEC, TALL) else bank for bank in banks[4:]]
        banks = [pltpu.with_memory_space_constraint(bank, pltpu.HBM) for bank in banks]
        results = finish(*step(*banks))
        return tuple(value.T if value.shape == (TALL, VEC) else value for value in results)

    grad_spec, shard_spec, full_spec = P("data", None, None), P(None, "data"), P(None, None)
    return jax.shard_map(local_step, mesh=mesh, in_specs=(grad_spec,) * 4 + (shard_spec,) * 12,
                         out_specs=(full_spec,) * 4 + (shard_spec,) * 12, check_vma=False)
```

time: 238 us -> 101 us (0.42)
  Pallas kernels: 0 us -> 99.8 us
  waiting for transfers between devices: 94.9 us -> 0 us
  blocking collectives: 69.6 us -> 0 us
  local copies, waits for them, and re-layouts: 24 us -> 0 us
  other arithmetic: 18.6 us -> 0 us
  between operations: 17.6 us -> 0.66 us
  starting transfers between devices: 12.6 us -> 0 us
    pallas_call x0 -> x2, Pallas kernels: none -> 99.8 us  [local_step(): results = finish(*step(*banks))]
    all_to_all x4 -> x0, waiting for transfers between devices: 67.3 us -> none  [local_step(): received = lax.all_to_all(by_owner, 'data', 1, 1, tiled=True)]
    psum x2 -> x0, blocking collectives: 45.7 us -> none  [the longest x1 23.4 us: local_step(): norm_sums = lax.psum(part_sums, 'data')]
    all_gather x2 -> x0, waiting for transfers between devices: 27.5 us -> none  [local_step(): lax.all_gather(new_weight.astype(jnp.bfloat16), 'data', axis=1, tiled=True)]
    all_gather x2 -> x0, blocking collectives: 23.9 us -> none  [local_step(): lax.all_gather(new_weight.astype(jnp.bfloat16), 'data', axis=1, tiled=True)]
    unnamed x41 -> x0, local copies, waits for them, and re-layouts: 16.3 us -> none
    all_to_all x4 -> x0, starting transfers between devices: 12.5 us -> none  [local_step(): received = lax.all_to_all(by_owner, 'data', 1, 1, tiled=True)]
    reduce_sum x12 -> x0, other arithmetic: 11.7 us -> none  [the longest x4 5.59 us: local_step(): jnp.sum(result[0] * result[0], axis=1)]
  transfers between devices with their start and end apart: 6 -> 0, of which waited for: 4 -> 0; matrix products, arithmetic and copies ran while one was open for 10% -> 0% of each run, Pallas kernels for 0% -> 0%
where the time goes in v2:
time: 101 us; the launch traced here: 100 us
  Pallas kernels  99.8 us (99%)
    pallas_call x2, Pallas kernels, local_step(): results = finish(*step(*banks))  99.8 us

profile of v2, /device:TPU:0, one launch (start us, length us, event | category | flops | bytes accessed | tf_op | source)
XLA Modules:
  0.0 100.5 jit_solution(11603932933882300780)
XLA Ops:
  0.7 95.5 %lamb_step.1 = (bf16[64,16384]{1,0:T(8,128)(2,1)S(1)}, bf16[32,65536]{1,0:T(8,128)(2,1)S(1)}, bf16[16,512]{1,0:T(8,128)(2,1)S(1)}, bf16[146,128]{1,0:T(8,128)(2,...) custom-call(bf16[64,16384]{1,0:T(8,128)(2,1)} %bitcast.11, ...), custom_call_target="tpu_custom_call" | custom-call | tf_op jit(solution)/shard_map/lamb_step/pallas_call | solution.py:495
  96.1 4.3 %write_out.1 = (bf16[64,16384]{1,0:T(8,128)(2,1)}, bf16[32,65536]{1,0:T(8,128)(2,1)}, bf16[16,512]{1,0:T(8,128)(2,1)}, bf16[146,128]{1,0:T(8,128)(2,1)}, f32[64,...) custom-call(bf16[64,16384]{1,0:T(8,128)(2,1)S(1)} %get-tuple-element, ...), custom_call_target="tpu_custom_call" | custom-call | tf_op jit(solution)/shard_map/write_out/pallas_call | solution.py:495

commit v3 on v2

--- a/solution.py
+++ b/solution.py
@@ -21,6 +21,7 @@
 LANES = 128
 TALL = 16
 HALF = 64
+FIRST = 32
 VEC = 146
 VEC_PAD = 256
 ATTN_SHARD = 2048
@@ -82,9 +83,8 @@
     replicas, new_weights, new_firsts, new_seconds = refs[16:20], refs[20:24], refs[24:28], refs[28:32]
     (recv_attn, recv_mlp, recv_wide, recv_vec, part_attn, part_mlp, part_wide, part_vec,
      last_attn, last_mlp, last_wide, last_vec, sum_attn, sum_mlp, sum_wide, sum_vec, dir_attn, dir_mlp,
-     vec_in, vec_out, vec_rows, vec_columns, vec_row, all_wide, all_vec, start_tiles, attn_tiles, rest_tiles, row_acc,
-     state_sem, vec_sem, scatter_send, scatter_recv, last_send, last_recv, tile_send, tile_recv,
-     own_send, own_recv, pass_send, pass_recv, pair_send, pair_recv) = refs[32:]
+     vec_in, vec_out, vec_rows, vec_columns, vec_row, all_wide, all_vec, start_tiles, first_tiles, rest_tiles, row_acc,
+     load_sems, sent, tile_sent, scatter_recv, last_recv, tile_recv, own_recv, pass_recv, pair_recv) = refs[32:]
     me = lax.axis_index("data")
     core = me % 2
 
@@ -114,33 +114,33 @@
             return replicas[0].at[pl.ds(32 * half, 32), aligned(owner, ATTN_SHARD)]
         return (all_vec if half else all_wide).at[owner]
 
-    def remote(source, target, send_sem, recv_sem, device):
-        return pltpu.make_async_remote_copy(src_ref=source, dst_ref=target, send_sem=send_sem, recv_sem=recv_sem,
+    def send(source, target, send_sem, recv_sem, device):
+        copy = pltpu.make_async_remote_copy(src_ref=source, dst_ref=target, send_sem=send_sem, recv_sem=recv_sem,
                                             device_id=(device,), device_id_type=MESH)
-
-    sends = []
-
-    def send(*copy):
-        copy = remote(*copy)
         copy.start()
-        sends.append(copy)
         return copy
 
-    vec_load = pltpu.make_async_copy(grads[3], vec_in, vec_sem)
+    def bank_of(half, chunk):
+        return chunk + half if chunk == SMALL else chunk
+
+    def wait_bytes(ref, sem):
+        pltpu.make_async_copy(ref, ref, sem).wait()
+
+    vec_load = pltpu.make_async_copy(grads[3], vec_in, load_sems.at[8])
     vec_load.start()
-    own = {}
     for keep in range(2):
         for half in HALVES:
             for chunk in (MLP, ATTN, SMALL)[:3 - half]:
                 owner = me if keep else flip(me, NEAR[half][1])
-                own[half, keep, chunk] = pltpu.make_async_copy(
-                    grad_chunk(half, owner, chunk), recv_chunk(half, keep, 0, chunk), scatter_recv.at[half, keep, 0, chunk])
-                own[half, keep, chunk].start()
-    loads = []
-    for source, target in ((weights, new_weights), (firsts, new_firsts), (seconds, new_seconds)):
+                pltpu.make_async_copy(grad_chunk(half, owner, chunk), recv_chunk(half, keep, 0, chunk),
+                                      scatter_recv.at[half, keep, chunk]).start()
+    small_loads = []
+    for index, (source, target) in enumerate(((weights, new_weights), (firsts, new_firsts), (seconds, new_seconds))):
         for bank in range(4):
-            loads.append(pltpu.make_async_copy(source[bank], target[bank], state_sem.at[len(loads)]))
-            loads[-1].start()
+            copy = pltpu.make_async_copy(source[bank], target[bank], load_sems.at[bank if bank < 2 else 2 * index + bank])
+            copy.start()
+            if bank >= 2:
+                small_loads.append(copy)
 
     barrier = pltpu.get_barrier_semaphore()
     near = (1, 2, 3, 4, 5)
@@ -155,7 +155,7 @@
                 owner = target if keep else flip(target, NEAR[half][1])
                 index = 1 if slot == 0 else 2 + core
                 send(grad_chunk(half, owner, chunk), recv_chunk(half, keep, index, chunk),
-                     scatter_send.at[half, keep, slot, chunk], scatter_recv.at[half, keep, index, chunk], target)
+                     sent.at[0, bank_of(half, chunk)], scatter_recv.at[half, keep, chunk], target)
 
     scatter(0, MLP)
     scatter(0, ATTN)
@@ -192,12 +192,11 @@
 
     def exchange(tiles, which, value):
         tiles[me] = value
-        return [send(tiles.at[me], tiles.at[me], tile_send.at[which, mask], tile_recv.at[which, mask], flip(me, mask))
-                for mask in FAR_FIRST]
-
-    def collect(tiles, copies):
-        for copy in copies:
-            copy.wait_recv()
+        for mask in FAR_FIRST:
+            send(tiles.at[me], tiles.at[me], tile_sent.at[which], tile_recv.at[which], flip(me, mask))
+
+    def collect(tiles, which):
+        wait_bytes(tiles.at[pl.ds(0, len(FAR_FIRST))], tile_recv.at[which])
         return add_all([tiles[index] for index in range(8)])
 
     def by_rows(first, groups, columns, step):
@@ -214,8 +213,10 @@
     def square_of(ref):
         return lambda place: fold(ref[place] * ref[place])
 
-    for load in loads:
-        load.wait()
+    for buffer, sem in ((recv_attn, load_sems.at[ATTN]), (recv_mlp, load_sems.at[MLP])):
+        wait_bytes(buffer.at[:, :, pl.ds(0, 3)], sem)
+    for copy in small_loads:
+        copy.wait()
     row_acc[...] = jnp.zeros_like(row_acc)
     by_rows(0, 8, ATTN_SHARD, square_of(new_weights[0]))
     by_rows(HALF, 4, MLP_SHARD, square_of(new_weights[1]))
@@ -232,12 +233,11 @@
         return init
 
     def gather_sum(half, keep, chunk):
-        if (half, keep, chunk) in own:
-            own[half, keep, chunk].wait()
-        for slot in range(1, 4):
-            place = recv_chunk(half, keep, slot, chunk)
-            remote(place, place, scatter_send.at[half, keep, 0, chunk], scatter_recv.at[half, keep, slot, chunk],
-                   flip(me, PEER)).wait_recv()
+        if chunk == SMALL:
+            arrived = recv_vec.at[keep, pl.ds(1, 3)] if half else recv_wide.at[keep]
+        else:
+            arrived = (recv_attn, recv_mlp)[chunk].at[half, keep]
+        wait_bytes(arrived, scatter_recv.at[half, keep, chunk])
         target = sum_chunk(half, chunk, (sum_attn, sum_mlp, sum_wide, sum_vec) if keep else parts)
         sources = [recv_chunk(half, keep, slot, chunk) for slot in range(4)]
         if chunk == SMALL:
@@ -259,7 +259,7 @@
         for half in HALVES:
             last[half, chunk] = send(
                 sum_chunk(half, chunk, parts), sum_chunk(half, chunk, lasts),
-                last_send.at[half, chunk], last_recv.at[half, chunk], flip(me, NEAR[half][1]))
+                sent.at[0, bank_of(half, chunk)], last_recv.at[half, chunk], flip(me, NEAR[half][1]))
     for chunk in (MLP, ATTN, SMALL):
         for half in HALVES:
             gather_sum(half, 1, chunk)
@@ -284,8 +284,8 @@
 
             square = by_blocks(chunk, step, square)
 
-    start = collect(start_tiles, exchange(start_tiles, 0, tile_of(
-        [weight_lanes, weight_low, weight_high, jnp.sum(square, axis=0, keepdims=True)])))
+    exchange(start_tiles, 0, tile_of([weight_lanes, weight_low, weight_high, jnp.sum(square, axis=0, keepdims=True)]))
+    start = collect(start_tiles, 0)
     square = jnp.sum(jnp.sum(start[3:4, :], axis=1, keepdims=True), axis=0, keepdims=True)
     clip = jnp.minimum(1.0, (8.0 * MAX_NORM) / jnp.sqrt(jnp.broadcast_to(square, (8, LANES)))) * 0.125
     clip_block = jnp.concatenate([clip] * (STEP // LANES), axis=1)
@@ -326,15 +326,15 @@
         new_seconds[bank][...] = new_second
         return direction(new_first, new_second, weight)
 
-    for half in HALVES:
-        update(ATTN, half)
-    attn_copies = exchange(attn_tiles, 1, tile_of([lanes_of(0, HALF)]))
+    update(ATTN, 0)
+    exchange(first_tiles, 1, tile_of([lanes_of(0, FIRST)]))
+    update(ATTN, 1)
     for half in HALVES:
         update(MLP, half)
     wide_dir = update_small(2, wide_total, wide_weight)
     vec_dir = update_small(3, vec_total, vec_weight)
     row_acc[96:112, 0:HALF] = wide_dir * wide_dir
-    rest_copies = exchange(rest_tiles, 2, tile_of([lanes_of(HALF, LANES), *vec_lanes(vec_dir * vec_dir)]))
+    exchange(rest_tiles, 2, tile_of([lanes_of(FIRST, LANES), *vec_lanes(vec_dir * vec_dir)]))
     for bank in (ATTN, MLP):
         for half in HALVES:
             store_moments(bank, half)
@@ -343,14 +343,15 @@
 
     def send_own(half, chunk, way):
         place = replica_chunk(half, me, chunk)
-        own_copies[half, chunk, way] = send(place, place, own_send.at[half, chunk, way], own_recv.at[half, chunk, way],
-                                            flip(me, (PEER, ALONG_X, ALONG_Y)[way]))
+        bank = bank_of(half, chunk)
+        recv_sem = own_recv.at[half, chunk, way - 1] if way else pair_recv.at[bank]
+        own_copies[half, chunk, way] = send(place, place, sent.at[1, bank], recv_sem, flip(me, (PEER, ALONG_X, ALONG_Y)[way]))
 
     def spread_ratio(first, last, ratio):
         row_acc[first:last, :] = jnp.broadcast_to(
             jnp.sum(jnp.where(eye[first:last, :], ratio[0:1, :], 0.0), axis=1, keepdims=True), (last - first, LANES))
 
-    def new_weight(bank, half):
+    def new_weight(bank, half, ways):
         rows, columns = SHAPES[bank]
 
         def step(place, carry):
@@ -364,16 +365,16 @@
             return carry
 
         by_blocks(bank, step, 0)
-        send_own(half, bank, 1 + half)
-        send_own(half, bank, 0)
-
-    spread_ratio(0, HALF, weight_norms / jnp.sqrt(collect(attn_tiles, attn_copies)))
+        for way in ways:
+            send_own(half, bank, way)
+
+    spread_ratio(0, FIRST, weight_norms / jnp.sqrt(collect(first_tiles, 1)))
+    new_weight(ATTN, 0, (1, 2, 0))
+    ratio = weight_norms / jnp.sqrt(collect(rest_tiles, 2))
+    spread_ratio(FIRST, LANES, ratio)
+    new_weight(ATTN, 1, (2, 0))
     for half in HALVES:
-        new_weight(ATTN, half)
-    ratio = weight_norms / jnp.sqrt(collect(rest_tiles, rest_copies))
-    spread_ratio(HALF, LANES, ratio)
-    for half in HALVES:
-        new_weight(MLP, half)
+        new_weight(MLP, half, (1 + half, 0))
     value = wide_weight - row_acc[96:112, 0:HALF] * wide_dir
     new_weights[2][...] = value
     all_wide[me] = jnp.concatenate([value, value], axis=1).astype(jnp.bfloat16)
@@ -387,16 +388,15 @@
     for half in HALVES:
         send_own(half, SMALL, 1 + half)
         send_own(half, SMALL, 0)
-    for chunk in (ATTN, MLP, SMALL):
+    send_own(1, ATTN, 1)
+    for chunk in (MLP, SMALL):
         for half in HALVES:
             send_own(half, chunk, 2 - half)
 
-    pairs = {}
-
-    def send_pair(half, owner, chunk, slot):
+    def send_pair(half, owner, chunk):
         place = replica_chunk(half, owner, chunk)
-        pairs[half, chunk, slot] = send(
-            place, place, pair_send.at[half, chunk, slot], pair_recv.at[half, chunk, slot], flip(me, PEER))
+        bank = bank_of(half, chunk)
+        send(place, place, sent.at[1, bank], pair_recv.at[bank], flip(me, PEER))
 
     passed = {}
     for chunk in (SMALL, MLP, ATTN):
@@ -404,22 +404,20 @@
             own_copies[half, chunk, 1 + half].wait_recv()
             owner = flip(me, NEAR[half][0])
             place = replica_chunk(half, owner, chunk)
-            passed[half, chunk] = send(place, place, pass_send.at[half, chunk], pass_recv.at[half, chunk],
+            passed[half, chunk] = send(place, place, sent.at[1, bank_of(half, chunk)], pass_recv.at[half, chunk],
                                        flip(me, NEAR[half][1]))
-            send_pair(half, owner, chunk, 0)
+            send_pair(half, owner, chunk)
     for chunk in (ATTN, MLP, SMALL):
         for half in HALVES:
             own_copies[half, chunk, 2 - half].wait_recv()
-            send_pair(half, flip(me, NEAR[half][1]), chunk, 1)
+            send_pair(half, flip(me, NEAR[half][1]), chunk)
     for chunk in (SMALL, MLP, ATTN):
         for half in HALVES:
             passed[half, chunk].wait_recv()
-            send_pair(half, flip(me, ALONG_X + ALONG_Y), chunk, 2)
-            if chunk == SMALL:
-                own_copies[half, chunk, 0].wait_recv()
-                for slot in range(3):
-                    pairs[half, chunk, slot].wait_recv()
+            send_pair(half, flip(me, ALONG_X + ALONG_Y), chunk)
         if chunk == SMALL:
+            for half, buffer in enumerate((all_wide, all_vec)):
+                wait_bytes(buffer.at[pl.ds(0, 4)], pair_recv.at[SMALL + half])
             low_lanes = lax.broadcasted_iota(jnp.int32, (TALL, LANES), 1) < HALF
             for index in range(4):
                 left, right = (all_wide[2 * index + k].astype(jnp.float32) for k in range(2))
@@ -428,18 +426,20 @@
                 vec_columns[pl.ds(TALL * index, TALL), :] = all_vec[index].astype(jnp.float32)
             vec_rows[...] = vec_columns[...].T
             replicas[3][...] = vec_rows[0:VEC, :].astype(jnp.bfloat16)
-    for chunk in (ATTN, MLP):
-        for half in HALVES:
-            own_copies[half, chunk, 0].wait_recv()
-            for slot in range(3):
-                pairs[half, chunk, slot].wait_recv()
-    for copy in sends:
-        copy.wait_send()
+    for bank in (ATTN, MLP):
+        wait_bytes(replicas[bank].at[:, pl.ds(0, LENGTHS[bank] // 2)], pair_recv.at[bank])
+        wait_bytes(replicas[bank], sent.at[0, bank])
+        wait_bytes(replicas[bank].at[:, pl.ds(0, len(FAR_FIRST) * SHARDS[bank][1])], sent.at[1, bank])
+    for half, buffer in enumerate((all_wide, all_vec)):
+        wait_bytes(buffer, sent.at[0, SMALL + half])
+        wait_bytes(buffer.at[pl.ds(0, len(FAR_FIRST))], sent.at[1, SMALL + half])
+    for which, tiles in enumerate((start_tiles, first_tiles, rest_tiles)):
+        wait_bytes(tiles.at[pl.ds(0, len(FAR_FIRST))], tile_sent.at[which])
 
 
 def write_out(*refs):
     count = (len(refs) - 1) // 2
-    copies = [pltpu.make_async_copy(refs[k], refs[count + k], refs[-1].at[k]) for k in range(count)]
+    copies = [pltpu.make_async_copy(refs[k], refs[count + k], refs[-1]) for k in range(count)]
     for copy in copies:
         copy.start()
     for copy in copies:
@@ -465,8 +465,7 @@
         pltpu.VMEM((VEC_PAD, LANES), f32), pltpu.VMEM((LANES, VEC_PAD), f32), pltpu.VMEM((8, VEC_PAD), f32),
         pltpu.VMEM((8, TALL, LANES), bf16), pltpu.VMEM((8, TALL, VEC_PAD), bf16),
         *[pltpu.VMEM((8, 8, LANES), f32)] * 3, pltpu.VMEM((LANES, LANES), f32),
-        dma((12,)), dma, dma((2, 2, 3, 3)), dma((2, 2, 4, 3)), dma((2, 3)), dma((2, 3)), dma((3, 8)), dma((3, 8)),
-        dma((2, 3, 3)), dma((2, 3, 3)), dma((2, 3)), dma((2, 3)), dma((2, 3, 3)), dma((2, 3, 3)),
+        dma((9,)), dma((2, 4)), dma((3,)), dma((2, 2, 3)), dma((2, 3)), dma((3,)), dma((2, 3, 2)), dma((2, 3)), dma((4,)),
     ]
     count = len(shapes)
     anywhere = [pl.BlockSpec(memory_space=pl.ANY)] * count
@@ -484,7 +483,7 @@
         out_shape=shapes,
         in_specs=anywhere,
         out_specs=anywhere,
-        scratch_shapes=[dma((count,))],
+        scratch_shapes=[dma],
         compiler_params=pltpu.CompilerParams(vmem_limit_bytes=MIB),
         name="write_out",
     )

time: 101 us -> 98.5 us (0.975)
  Pallas kernels: 99.8 us -> 97.7 us
    pallas_call x2, Pallas kernels: 99.8 us -> 97.7 us  [local_step(): results = finish(*step(*banks))]
where the time goes in v3:
time: 98.5 us; the launch traced here: 98.4 us
  Pallas kernels  97.7 us (99%)
    pallas_call x2, Pallas kernels, local_step(): results = finish(*step(*banks))  97.7 us

profile of v3, /device:TPU:0, one launch (start us, length us, event | category | flops | bytes accessed | tf_op | source)
XLA Modules:
  0.0 98.4 jit_solution(10212645967071953342)
XLA Ops:
  0.7 93.5 %lamb_step.1 = (bf16[64,16384]{1,0:T(8,128)(2,1)S(1)}, bf16[32,65536]{1,0:T(8,128)(2,1)S(1)}, bf16[16,512]{1,0:T(8,128)(2,1)S(1)}, bf16[146,128]{1,0:T(8,128)(2,...) custom-call(bf16[64,16384]{1,0:T(8,128)(2,1)} %bitcast.11, ...), custom_call_target="tpu_custom_call" | custom-call | tf_op jit(solution)/shard_map/lamb_step/pallas_call | solution.py:494
  94.2 4.2 %write_out.1 = (bf16[64,16384]{1,0:T(8,128)(2,1)}, bf16[32,65536]{1,0:T(8,128)(2,1)}, bf16[16,512]{1,0:T(8,128)(2,1)}, bf16[146,128]{1,0:T(8,128)(2,1)}, f32[64,...) custom-call(bf16[64,16384]{1,0:T(8,128)(2,1)S(1)} %get-tuple-element, ...), custom_call_target="tpu_custom_call" | custom-call | tf_op jit(solution)/shard_map/write_out/pallas_call | solution.py:494

commit v4 on v3

--- a/solution.py
+++ b/solution.py
@@ -33,10 +33,12 @@
 LENGTHS = (16384, 65536, BLOCK, LANES)
 SHARDS = ((HALF, ATTN_SHARD), (32, MLP_SHARD), (TALL, HALF), (TALL, VEC))
 ATTN, MLP, SMALL = range(3)
+BIG = (ATTN, MLP)
 HALVES = range(2)
 SHAPES = ((32, ATTN_SHARD), (TALL, MLP_SHARD))
 PEER, ALONG_X, ALONG_Y = 1, 2, 4
 NEAR = ((ALONG_X, ALONG_Y), (ALONG_Y, ALONG_X))
+WIDE_LANES = (LANES, LANES + HALF)
 FAR_FIRST = tuple(reversed(range(1, 8)))
 
 
@@ -81,38 +83,26 @@
 def kernel(*refs):
     grads, weights, firsts, seconds = refs[0:4], refs[4:8], refs[8:12], refs[12:16]
     replicas, new_weights, new_firsts, new_seconds = refs[16:20], refs[20:24], refs[24:28], refs[28:32]
-    (recv_attn, recv_mlp, recv_wide, recv_vec, part_attn, part_mlp, part_wide, part_vec,
-     last_attn, last_mlp, last_wide, last_vec, sum_attn, sum_mlp, sum_wide, sum_vec, dir_attn, dir_mlp,
-     vec_in, vec_out, vec_rows, vec_columns, vec_row, all_wide, all_vec, start_tiles, first_tiles, rest_tiles, row_acc,
-     load_sems, sent, tile_sent, scatter_recv, last_recv, tile_recv, own_recv, pass_recv, pair_recv) = refs[32:]
+    (recv_attn, recv_mlp, recv_small, part_attn, part_mlp, part_small, last_attn, last_mlp, last_small,
+     sum_attn, sum_mlp, sum_small, dir_attn, dir_mlp, vec_in, wide_in, small_out, all_small,
+     vec_rows, vec_columns, vec_row, start_tiles, first_tiles, rest_tiles, row_acc,
+     load_sems, sent, tile_sent, scatter_recv, small_recv, last_recv, tile_recv, own_recv, pass_recv, pair_recv) = refs[32:]
+    recvs, parts, lasts = (recv_attn, recv_mlp), (part_attn, part_mlp), (last_attn, last_mlp)
     me = lax.axis_index("data")
     core = me % 2
 
     def grad_chunk(half, owner, chunk):
-        if chunk == MLP:
-            return grads[1].at[pl.ds(TALL * half, TALL), aligned(owner, MLP_SHARD)]
-        if chunk == ATTN:
-            return grads[0].at[pl.ds(32 * half, 32), aligned(owner, ATTN_SHARD)]
-        return vec_out.at[aligned(owner, TALL), :] if half else grads[2].at[:, aligned(owner // 2, LANES)]
-
-    def recv_chunk(half, keep, slot, chunk):
-        if chunk == SMALL:
-            return (recv_vec if half else recv_wide).at[keep, slot]
-        return (recv_attn, recv_mlp)[chunk].at[half, keep, slot]
-
-    def sum_chunk(half, chunk, buffers):
-        if chunk == SMALL:
-            return buffers[3] if half else buffers[2]
-        return buffers[chunk].at[half]
-
-    parts, lasts = (part_attn, part_mlp, part_wide, part_vec), (last_attn, last_mlp, last_wide, last_vec)
+        rows, columns = SHAPES[chunk]
+        return grads[chunk].at[pl.ds(rows * half, rows), aligned(owner, columns)]
 
     def replica_chunk(half, owner, chunk):
-        if chunk == MLP:
-            return replicas[1].at[pl.ds(TALL * half, TALL), aligned(owner, MLP_SHARD)]
-        if chunk == ATTN:
-            return replicas[0].at[pl.ds(32 * half, 32), aligned(owner, ATTN_SHARD)]
-        return (all_vec if half else all_wide).at[owner]
+        rows, columns = SHAPES[chunk]
+        return replicas[chunk].at[pl.ds(rows * half, rows), aligned(owner, columns)]
+
+    along_x, along_y = flip(me, ALONG_X), flip(me, ALONG_Y)
+    small_near = (along_x * (1 - core) + along_y * core, along_y * (1 - core) + along_x * core)
+    peer = flip(me, PEER)
+    peer_next = flip(peer, ALONG_X) * (1 - core) + flip(peer, ALONG_Y) * core
 
     def send(source, target, send_sem, recv_sem, device):
         copy = pltpu.make_async_remote_copy(src_ref=source, dst_ref=target, send_sem=send_sem, recv_sem=recv_sem,
@@ -120,55 +110,69 @@
         copy.start()
         return copy
 
-    def bank_of(half, chunk):
-        return chunk + half if chunk == SMALL else chunk
-
     def wait_bytes(ref, sem):
         pltpu.make_async_copy(ref, ref, sem).wait()
-
-    vec_load = pltpu.make_async_copy(grads[3], vec_in, load_sems.at[8])
-    vec_load.start()
-    for keep in range(2):
-        for half in HALVES:
-            for chunk in (MLP, ATTN, SMALL)[:3 - half]:
-                owner = me if keep else flip(me, NEAR[half][1])
-                pltpu.make_async_copy(grad_chunk(half, owner, chunk), recv_chunk(half, keep, 0, chunk),
-                                      scatter_recv.at[half, keep, chunk]).start()
-    small_loads = []
-    for index, (source, target) in enumerate(((weights, new_weights), (firsts, new_firsts), (seconds, new_seconds))):
-        for bank in range(4):
-            copy = pltpu.make_async_copy(source[bank], target[bank], load_sems.at[bank if bank < 2 else 2 * index + bank])
-            copy.start()
-            if bank >= 2:
-                small_loads.append(copy)
 
     barrier = pltpu.get_barrier_semaphore()
     near = (1, 2, 3, 4, 5)
     for mask in near:
         pl.semaphore_signal(barrier, inc=1, device_id=(flip(me, mask),), device_id_type=MESH)
+
+    small_loads = [pltpu.make_async_copy(grads[2], wide_in, load_sems.at[2]),
+                   pltpu.make_async_copy(grads[3], vec_in, load_sems.at[3])]
+    for copy in small_loads:
+        copy.start()
+    for keep in range(2):
+        for half in HALVES:
+            for chunk in (MLP, ATTN):
+                owner = me if keep else flip(me, NEAR[half][1])
+                pltpu.make_async_copy(grad_chunk(half, owner, chunk), recvs[chunk].at[half, keep, 0],
+                                      scatter_recv.at[half, keep, chunk]).start()
+    state_loads = []
+    for index, (source, target) in enumerate(((weights, new_weights), (firsts, new_firsts), (seconds, new_seconds))):
+        for bank in range(4):
+            copy = pltpu.make_async_copy(source[bank], target[bank], load_sems.at[bank if bank < 2 else 2 * index + bank + 2])
+            copy.start()
+            if bank >= 2:
+                state_loads.append(copy)
     pl.semaphore_wait(barrier, len(near))
 
     def scatter(keep, chunk):
-        for slot in range(3):
+        for slot in (1, 2, 0):
             for half in HALVES:
-                target = flip(me, PEER) if slot == 0 else flip(me, NEAR[half][0]) // 2 * 2 + slot - 1
+                target = peer if slot == 0 else flip(me, NEAR[half][0]) // 2 * 2 + slot - 1
                 owner = target if keep else flip(target, NEAR[half][1])
-                index = 1 if slot == 0 else 2 + core
-                send(grad_chunk(half, owner, chunk), recv_chunk(half, keep, index, chunk),
-                     sent.at[0, bank_of(half, chunk)], scatter_recv.at[half, keep, chunk], target)
+                send(grad_chunk(half, owner, chunk), recvs[chunk].at[half, keep, 1 if slot == 0 else 2 + core],
+                     sent.at[0, chunk], scatter_recv.at[half, keep, chunk], target)
 
     scatter(0, MLP)
     scatter(0, ATTN)
-    vec_load.wait()
+    for copy in small_loads:
+        copy.wait()
     vec_rows[...] = jnp.zeros_like(vec_rows)
     vec_rows[0:VEC, :] = vec_in[...].astype(jnp.float32)
-    vec_out[...] = vec_rows[...].T.astype(jnp.bfloat16)
-    recv_vec[0, 0] = vec_out[aligned(flip(me, NEAR[1][1]), TALL), :]
-    recv_vec[1, 0] = vec_out[aligned(me, TALL), :]
-    scatter(0, SMALL)
+    vec_columns[...] = vec_rows[...].T
+
+    def small_message(wide, vec):
+        pad = jnp.zeros((TALL, VEC_PAD - VEC - HALF), jnp.float32)
+        return jnp.concatenate([vec[:, 0:LANES], wide, vec[:, LANES:VEC], pad], axis=1).astype(jnp.bfloat16)
+
+    def small_parts(message):
+        vec = jnp.concatenate([message[:, 0:LANES], message[:, WIDE_LANES[1]:HALF + VEC]], axis=1)
+        return message[:, slice(*WIDE_LANES)], vec
+
+    wide_grad = wide_in[...].astype(jnp.float32)
+    for owner in range(8):
+        small_out[owner] = small_message(
+            wide_grad[:, HALF * owner:HALF * owner + HALF], vec_columns[TALL * owner:TALL * owner + TALL, 0:VEC])
+    for keep in range(2):
+        recv_small[keep, 0] = small_out[me if keep else small_near[1]]
+        places = [(along_x // 2 * 2, ALONG_Y), (along_y // 2 * 2 + 1, ALONG_X)]
+        targets = [(target, target if keep else flip(target, way), 2 + core) for target, way in places]
+        for target, owner, slot in [*targets, (peer, peer if keep else peer_next, 1)]:
+            send(small_out.at[owner], recv_small.at[keep, slot], sent.at[0, SMALL], small_recv.at[keep], target)
     scatter(1, MLP)
     scatter(1, ATTN)
-    scatter(1, SMALL)
 
     row = lax.broadcasted_iota(jnp.int32, (LANES, LANES), 0)
     lane = lax.broadcasted_iota(jnp.int32, (LANES, LANES), 1)
@@ -215,7 +219,7 @@
 
     for buffer, sem in ((recv_attn, load_sems.at[ATTN]), (recv_mlp, load_sems.at[MLP])):
         wait_bytes(buffer.at[:, :, pl.ds(0, 3)], sem)
-    for copy in small_loads:
+    for copy in state_loads:
         copy.wait()
     row_acc[...] = jnp.zeros_like(row_acc)
     by_rows(0, 8, ATTN_SHARD, square_of(new_weights[0]))
@@ -233,49 +237,44 @@
         return init
 
     def gather_sum(half, keep, chunk):
-        if chunk == SMALL:
-            arrived = recv_vec.at[keep, pl.ds(1, 3)] if half else recv_wide.at[keep]
-        else:
-            arrived = (recv_attn, recv_mlp)[chunk].at[half, keep]
-        wait_bytes(arrived, scatter_recv.at[half, keep, chunk])
-        target = sum_chunk(half, chunk, (sum_attn, sum_mlp, sum_wide, sum_vec) if keep else parts)
-        sources = [recv_chunk(half, keep, slot, chunk) for slot in range(4)]
-        if chunk == SMALL:
-            target[...] = add_all([source[...].astype(jnp.float32) for source in sources])
-            return
+        source, target = recvs[chunk].at[half, keep], ((sum_attn, sum_mlp) if keep else parts)[chunk].at[half]
+        wait_bytes(source, scatter_recv.at[half, keep, chunk])
 
         def step(place, carry):
-            value = [source[place].astype(jnp.float32) for source in sources]
+            value = [source[(slot, *place)].astype(jnp.float32) for slot in range(4)]
             target[place] = (value[0] + value[1]) + (value[2] + value[3])
             return carry
 
         by_blocks(chunk, step, 0)
 
+    def gather_small(keep, target):
+        wait_bytes(recv_small.at[keep, pl.ds(1, 3)], small_recv.at[keep])
+        target[...] = add_all([recv_small[keep, slot].astype(jnp.float32) for slot in range(4)])
+
     last = {}
-    for chunk in (MLP, ATTN, SMALL):
+    for chunk in (MLP, ATTN):
         for half in HALVES:
             gather_sum(half, 0, chunk)
-    for chunk in (SMALL, MLP, ATTN):
-        for half in HALVES:
-            last[half, chunk] = send(
-                sum_chunk(half, chunk, parts), sum_chunk(half, chunk, lasts),
-                sent.at[0, bank_of(half, chunk)], last_recv.at[half, chunk], flip(me, NEAR[half][1]))
-    for chunk in (MLP, ATTN, SMALL):
+    gather_small(0, part_small)
+    last_small_copy = send(part_small, last_small, sent.at[0, SMALL], last_recv.at[0, SMALL], small_near[1])
+    for chunk in (MLP, ATTN):
+        for half in HALVES:
+            last[half, chunk] = send(parts[chunk].at[half], lasts[chunk].at[half], sent.at[0, chunk],
+                                     last_recv.at[half, chunk], flip(me, NEAR[half][1]))
+    for chunk in (MLP, ATTN):
         for half in HALVES:
             gather_sum(half, 1, chunk)
-
-    for half in HALVES:
-        last[half, SMALL].wait_recv()
-    wide_total = sum_wide[...] + last_wide[...]
-    wide_total = jnp.where(core == 0, wide_total[:, 0:HALF], wide_total[:, HALF:LANES])
-    vec_total = (sum_vec[...] + last_vec[...])[:, 0:VEC]
+    gather_small(1, sum_small)
+
+    last_small_copy.wait_recv()
+    wide_total, vec_total = small_parts(sum_small[...] + last_small[...])
     square = fold(jnp.concatenate([wide_total * wide_total, jnp.zeros((TALL, HALF), jnp.float32)], axis=1))
     low, high = vec_lanes(vec_total * vec_total)
     square = square + tile_of([low, high])
     for chunk in (MLP, ATTN):
         for half in HALVES:
             last[half, chunk].wait_recv()
-            total, rest = sum_chunk(half, chunk, (sum_attn, sum_mlp)), sum_chunk(half, chunk, lasts)
+            total, rest = (sum_attn, sum_mlp)[chunk].at[half], lasts[chunk].at[half]
 
             def step(place, acc):
                 value = total[place] + rest[place]
@@ -342,10 +341,9 @@
     own_copies = {}
 
     def send_own(half, chunk, way):
-        place = replica_chunk(half, me, chunk)
-        bank = bank_of(half, chunk)
-        recv_sem = own_recv.at[half, chunk, way - 1] if way else pair_recv.at[bank]
-        own_copies[half, chunk, way] = send(place, place, sent.at[1, bank], recv_sem, flip(me, (PEER, ALONG_X, ALONG_Y)[way]))
+        place = all_small.at[me] if chunk == SMALL else replica_chunk(half, me, chunk)
+        recv_sem = own_recv.at[half, chunk, way - 1] if way else pair_recv.at[chunk]
+        own_copies[half, chunk, way] = send(place, place, sent.at[1, chunk], recv_sem, flip(me, (PEER, ALONG_X, ALONG_Y)[way]))
 
     def spread_ratio(first, last, ratio):
         row_acc[first:last, :] = jnp.broadcast_to(
@@ -377,62 +375,58 @@
         new_weight(MLP, half, (1 + half, 0))
     value = wide_weight - row_acc[96:112, 0:HALF] * wide_dir
     new_weights[2][...] = value
-    all_wide[me] = jnp.concatenate([value, value], axis=1).astype(jnp.bfloat16)
+    wide_value = value
     vec_row[0:1, 0:LANES] = ratio[1:2, :]
     vec_row[0:1, LANES:VEC_PAD] = ratio[2:3, :]
     value = vec_weight - vec_row[0:1, 0:VEC] * vec_dir
     new_weights[3][...] = value
-    vec_columns[0:TALL, :] = jnp.zeros((TALL, VEC_PAD), jnp.float32)
-    vec_columns[0:TALL, 0:VEC] = value
-    all_vec[me] = vec_columns[0:TALL, :].astype(jnp.bfloat16)
+    all_small[me] = small_message(wide_value, value)
+    for way in (1, 2, 0):
+        send_own(0, SMALL, way)
+    send_own(1, ATTN, 1)
     for half in HALVES:
-        send_own(half, SMALL, 1 + half)
-        send_own(half, SMALL, 0)
-    send_own(1, ATTN, 1)
-    for chunk in (MLP, SMALL):
-        for half in HALVES:
-            send_own(half, chunk, 2 - half)
-
-    def send_pair(half, owner, chunk):
-        place = replica_chunk(half, owner, chunk)
-        bank = bank_of(half, chunk)
-        send(place, place, sent.at[1, bank], pair_recv.at[bank], flip(me, PEER))
-
+        send_own(half, MLP, 2 - half)
+
+    def send_pair(place, chunk):
+        send(place, place, sent.at[1, chunk], pair_recv.at[chunk], peer)
+
+    for way in (1, 2):
+        own_copies[0, SMALL, way].wait_recv()
+    place = all_small.at[small_near[0]]
+    passed_small = send(place, place, sent.at[1, SMALL], pass_recv.at[0, SMALL], small_near[1])
+    for owner in small_near:
+        send_pair(all_small.at[owner], SMALL)
     passed = {}
-    for chunk in (SMALL, MLP, ATTN):
+    for chunk in (MLP, ATTN):
         for half in HALVES:
             own_copies[half, chunk, 1 + half].wait_recv()
-            owner = flip(me, NEAR[half][0])
-            place = replica_chunk(half, owner, chunk)
-            passed[half, chunk] = send(place, place, sent.at[1, bank_of(half, chunk)], pass_recv.at[half, chunk],
-                                       flip(me, NEAR[half][1]))
-            send_pair(half, owner, chunk)
-    for chunk in (ATTN, MLP, SMALL):
+            place = replica_chunk(half, flip(me, NEAR[half][0]), chunk)
+            passed[half, chunk] = send(place, place, sent.at[1, chunk], pass_recv.at[half, chunk], flip(me, NEAR[half][1]))
+            send_pair(place, chunk)
+    for chunk in BIG:
         for half in HALVES:
             own_copies[half, chunk, 2 - half].wait_recv()
-            send_pair(half, flip(me, NEAR[half][1]), chunk)
-    for chunk in (SMALL, MLP, ATTN):
+            send_pair(replica_chunk(half, flip(me, NEAR[half][1]), chunk), chunk)
+    far = flip(me, ALONG_X + ALONG_Y)
+    passed_small.wait_recv()
+    send_pair(all_small.at[far], SMALL)
+    wait_bytes(all_small.at[pl.ds(0, 4)], pair_recv.at[SMALL])
+    wides, vecs = zip(*(small_parts(all_small[owner].astype(jnp.float32)) for owner in range(8)))
+    replicas[2][...] = jnp.concatenate(wides, axis=1).astype(jnp.bfloat16)
+    for owner in range(8):
+        vec_columns[TALL * owner:TALL * owner + TALL, 0:VEC] = vecs[owner]
+    vec_rows[...] = vec_columns[...].T
+    replicas[3][...] = vec_rows[0:VEC, :].astype(jnp.bfloat16)
+    for chunk in (MLP, ATTN):
         for half in HALVES:
             passed[half, chunk].wait_recv()
-            send_pair(half, flip(me, ALONG_X + ALONG_Y), chunk)
-        if chunk == SMALL:
-            for half, buffer in enumerate((all_wide, all_vec)):
-                wait_bytes(buffer.at[pl.ds(0, 4)], pair_recv.at[SMALL + half])
-            low_lanes = lax.broadcasted_iota(jnp.int32, (TALL, LANES), 1) < HALF
-            for index in range(4):
-                left, right = (all_wide[2 * index + k].astype(jnp.float32) for k in range(2))
-                replicas[2][:, pl.ds(LANES * index, LANES)] = jnp.where(low_lanes, left, right).astype(jnp.bfloat16)
-            for index in range(8):
-                vec_columns[pl.ds(TALL * index, TALL), :] = all_vec[index].astype(jnp.float32)
-            vec_rows[...] = vec_columns[...].T
-            replicas[3][...] = vec_rows[0:VEC, :].astype(jnp.bfloat16)
+            send_pair(replica_chunk(half, far, chunk), chunk)
     for bank in (ATTN, MLP):
         wait_bytes(replicas[bank].at[:, pl.ds(0, LENGTHS[bank] // 2)], pair_recv.at[bank])
         wait_bytes(replicas[bank], sent.at[0, bank])
         wait_bytes(replicas[bank].at[:, pl.ds(0, len(FAR_FIRST) * SHARDS[bank][1])], sent.at[1, bank])
-    for half, buffer in enumerate((all_wide, all_vec)):
-        wait_bytes(buffer, sent.at[0, SMALL + half])
-        wait_bytes(buffer.at[pl.ds(0, len(FAR_FIRST))], sent.at[1, SMALL + half])
+    wait_bytes(all_small, sent.at[0, SMALL])
+    wait_bytes(all_small.at[pl.ds(0, len(FAR_FIRST))], sent.at[1, SMALL])
     for which, tiles in enumerate((start_tiles, first_tiles, rest_tiles)):
         wait_bytes(tiles.at[pl.ds(0, len(FAR_FIRST))], tile_sent.at[which])
 
@@ -456,16 +450,16 @@
     def sums(*lead):
         return [pltpu.VMEM((*lead, *attn), f32), pltpu.VMEM((*lead, *mlp), f32)]
 
-    small_sums = [pltpu.VMEM((TALL, LANES), f32), pltpu.VMEM((TALL, VEC_PAD), f32)]
+    small = (TALL, VEC_PAD)
     scratch = [
-        pltpu.VMEM((2, 2, 4, *attn), bf16), pltpu.VMEM((2, 2, 4, *mlp), bf16),
-        pltpu.VMEM((2, 4, TALL, LANES), bf16), pltpu.VMEM((2, 4, TALL, VEC_PAD), bf16),
-        *sums(2), *small_sums, *sums(2), *small_sums, *sums(2), *small_sums, *sums(2),
-        pltpu.VMEM((VEC, LANES), bf16), pltpu.VMEM((LANES, VEC_PAD), bf16),
+        pltpu.VMEM((2, 2, 4, *attn), bf16), pltpu.VMEM((2, 2, 4, *mlp), bf16), pltpu.VMEM((2, 4, *small), bf16),
+        *sums(2), pltpu.VMEM(small, f32), *sums(2), pltpu.VMEM(small, f32), *sums(2), pltpu.VMEM(small, f32), *sums(2),
+        pltpu.VMEM((VEC, LANES), bf16), pltpu.VMEM((TALL, BLOCK), bf16), pltpu.VMEM((8, *small), bf16),
+        pltpu.VMEM((8, *small), bf16),
         pltpu.VMEM((VEC_PAD, LANES), f32), pltpu.VMEM((LANES, VEC_PAD), f32), pltpu.VMEM((8, VEC_PAD), f32),
-        pltpu.VMEM((8, TALL, LANES), bf16), pltpu.VMEM((8, TALL, VEC_PAD), bf16),
         *[pltpu.VMEM((8, 8, LANES), f32)] * 3, pltpu.VMEM((LANES, LANES), f32),
-        dma((9,)), dma((2, 4)), dma((3,)), dma((2, 2, 3)), dma((2, 3)), dma((3,)), dma((2, 3, 2)), dma((2, 3)), dma((4,)),
+        dma((10,)), dma((2, 3)), dma((3,)), dma((2, 2, 2)), dma((2,)), dma((2, 3)), dma((3,)), dma((2, 3, 2)), dma((2, 3)),
+        dma((3,)),
     ]
     count = len(shapes)
     anywhere = [pl.BlockSpec(memory_space=pl.ANY)] * count

time: 98.5 us -> 98.1 us (level)
  no operation moved by 1% of the time
where the time goes in v4:
time: 98.1 us; the launch traced here: 97.9 us
  Pallas kernels  97.2 us (99%)
    pallas_call x2, Pallas kernels, local_step(): results = finish(*step(*banks))  97.2 us

profile of v4, /device:TPU:0, one launch (start us, length us, event | category | flops | bytes accessed | tf_op | source)
XLA Modules:
  0.0 97.9 jit_solution(11075576528719247330)
XLA Ops:
  0.7 93.0 %lamb_step.1 = (bf16[64,16384]{1,0:T(8,128)(2,1)S(1)}, bf16[32,65536]{1,0:T(8,128)(2,1)S(1)}, bf16[16,512]{1,0:T(8,128)(2,1)S(1)}, bf16[146,128]{1,0:T(8,128)(2,...) custom-call(bf16[64,16384]{1,0:T(8,128)(2,1)} %bitcast.11, ...), custom_call_target="tpu_custom_call" | custom-call | tf_op jit(solution)/shard_map/lamb_step/pallas_call | solution.py:488
  93.7 4.2 %write_out.1 = (bf16[64,16384]{1,0:T(8,128)(2,1)}, bf16[32,65536]{1,0:T(8,128)(2,1)}, bf16[16,512]{1,0:T(8,128)(2,1)}, bf16[146,128]{1,0:T(8,128)(2,1)}, f32[64,...) custom-call(bf16[64,16384]{1,0:T(8,128)(2,1)S(1)} %get-tuple-element, ...), custom_call_target="tpu_custom_call" | custom-call | tf_op jit(solution)/shard_map/write_out/pallas_call | solution.py:488

commit v5 on v4

--- a/solution.py
+++ b/solution.py
@@ -22,6 +22,7 @@
 TALL = 16
 HALF = 64
 FIRST = 32
+EARLY = 1024
 VEC = 146
 VEC_PAD = 256
 ATTN_SHARD = 2048
@@ -84,9 +85,10 @@
     grads, weights, firsts, seconds = refs[0:4], refs[4:8], refs[8:12], refs[12:16]
     replicas, new_weights, new_firsts, new_seconds = refs[16:20], refs[20:24], refs[24:28], refs[28:32]
     (recv_attn, recv_mlp, recv_small, part_attn, part_mlp, part_small, last_attn, last_mlp, last_small,
-     sum_attn, sum_mlp, sum_small, dir_attn, dir_mlp, vec_in, wide_in, small_out, all_small,
+     sum_attn, sum_mlp, sum_small, dir_attn, dir_mlp, early_weight, early_dir, vec_in, wide_in, small_out, all_small,
      vec_rows, vec_columns, vec_row, start_tiles, first_tiles, rest_tiles, row_acc,
-     load_sems, sent, tile_sent, scatter_recv, small_recv, last_recv, tile_recv, own_recv, pass_recv, pair_recv) = refs[32:]
+     load_sems, sent, tile_sent, scatter_recv, small_recv, last_recv, tile_recv, own_recv, pass_recv, pair_recv,
+     early_sent, early_recv) = refs[32:]
     recvs, parts, lasts = (recv_attn, recv_mlp), (part_attn, part_mlp), (last_attn, last_mlp)
     me = lax.axis_index("data")
     core = me % 2
@@ -229,8 +231,8 @@
     weight_lanes = lanes_of(0, LANES)
     weight_low, weight_high = vec_lanes(vec_weight * vec_weight)
 
-    def by_blocks(chunk, step, init):
-        rows, columns = SHAPES[chunk]
+    def by_blocks(shape, step, init):
+        rows, columns = shape
         for r in range(0, rows, TALL):
             init = lax.fori_loop(0, columns // BLOCK, functools.partial(
                 lambda first, j, carry: step((pl.ds(first, TALL), aligned(j, BLOCK)), carry), r), init)
@@ -245,7 +247,7 @@
             target[place] = (value[0] + value[1]) + (value[2] + value[3])
             return carry
 
-        by_blocks(chunk, step, 0)
+        by_blocks(SHAPES[chunk], step, 0)
 
     def gather_small(keep, target):
         wait_bytes(recv_small.at[keep, pl.ds(1, 3)], small_recv.at[keep])
@@ -281,9 +283,17 @@
                 total[place] = value
                 return acc + fold(value * value)
 
-            square = by_blocks(chunk, step, square)
+            square = by_blocks(SHAPES[chunk], step, square)
 
     exchange(start_tiles, 0, tile_of([weight_lanes, weight_low, weight_high, jnp.sum(square, axis=0, keepdims=True)]))
+    late_rows = pl.ds(FIRST, FIRST)
+    early_columns = pl.ds(0, EARLY)
+
+    def send_early(kind, source, buffer):
+        for way, mask in enumerate((ALONG_X, ALONG_Y)):
+            send(source, buffer.at[way], early_sent.at[kind], early_recv.at[kind, way], flip(me, mask))
+
+    send_early(0, new_weights[ATTN].at[late_rows, early_columns], early_weight)
     start = collect(start_tiles, 0)
     square = jnp.sum(jnp.sum(start[3:4, :], axis=1, keepdims=True), axis=0, keepdims=True)
     clip = jnp.minimum(1.0, (8.0 * MAX_NORM) / jnp.sqrt(jnp.broadcast_to(square, (8, LANES)))) * 0.125
@@ -317,7 +327,7 @@
             new_seconds[bank][state] = new_second
             return carry
 
-        by_blocks(bank, step, 0)
+        by_blocks(SHAPES[bank], step, 0)
 
     def update_small(bank, total, weight):
         new_first, new_second = moments(new_firsts[bank][...], new_seconds[bank][...], total, clip[0:1, 0:1])
@@ -328,6 +338,7 @@
     update(ATTN, 0)
     exchange(first_tiles, 1, tile_of([lanes_of(0, FIRST)]))
     update(ATTN, 1)
+    send_early(1, dir_attn.at[1, :, early_columns], early_dir)
     for half in HALVES:
         update(MLP, half)
     wide_dir = update_small(2, wide_total, wide_weight)
@@ -342,6 +353,8 @@
 
     def send_own(half, chunk, way):
         place = all_small.at[me] if chunk == SMALL else replica_chunk(half, me, chunk)
+        if (half, chunk) == (1, ATTN) and way:
+            place = replicas[ATTN].at[late_rows, pl.ds(pl.multiple_of(me * ATTN_SHARD + EARLY, BLOCK), ATTN_SHARD - EARLY)]
         recv_sem = own_recv.at[half, chunk, way - 1] if way else pair_recv.at[chunk]
         own_copies[half, chunk, way] = send(place, place, sent.at[1, chunk], recv_sem, flip(me, (PEER, ALONG_X, ALONG_Y)[way]))
 
@@ -349,20 +362,25 @@
         row_acc[first:last, :] = jnp.broadcast_to(
             jnp.sum(jnp.where(eye[first:last, :], ratio[0:1, :], 0.0), axis=1, keepdims=True), (last - first, LANES))
 
-    def new_weight(bank, half, ways):
-        rows, columns = SHAPES[bank]
+    def form_weights(bank, half, owner, shape, weight, direct, result):
+        rows = SHAPES[bank][0]
 
         def step(place, carry):
             first = half * rows + place[0].start
             scale = jnp.concatenate([row_acc[HALF * bank + first:HALF * bank + first + TALL, :]] * (BLOCK // LANES), axis=1)
-            state = (pl.ds(first, TALL), place[1])
-            value = new_weights[bank][state] - scale * directions[bank].at[half][place]
-            new_weights[bank][state] = value
-            target = pl.ds(pl.multiple_of(me * columns + place[1].start, BLOCK), BLOCK)
+            value = weight[place] - scale * direct[place]
+            if result is not None:
+                result[place] = value
+            target = pl.ds(pl.multiple_of(owner * SHAPES[bank][1] + place[1].start, BLOCK), BLOCK)
             replicas[bank][pl.ds(first, TALL), target] = value.astype(jnp.bfloat16)
             return carry
 
-        by_blocks(bank, step, 0)
+        by_blocks(shape, step, 0)
+
+    def new_weight(bank, half, ways):
+        rows = SHAPES[bank][0]
+        mine = new_weights[bank].at[pl.ds(half * rows, rows)]
+        form_weights(bank, half, me, SHAPES[bank], mine, directions[bank].at[half], mine)
         for way in ways:
             send_own(half, bank, way)
 
@@ -370,6 +388,7 @@
     new_weight(ATTN, 0, (1, 2, 0))
     ratio = weight_norms / jnp.sqrt(collect(rest_tiles, 2))
     spread_ratio(FIRST, LANES, ratio)
+    wait_bytes(early_weight, early_sent.at[0])
     new_weight(ATTN, 1, (2, 0))
     for half in HALVES:
         new_weight(MLP, half, (1 + half, 0))
@@ -387,6 +406,11 @@
     for half in HALVES:
         send_own(half, MLP, 2 - half)
 
+    for way, owner in enumerate((along_x, along_y)):
+        for kind, buffer in enumerate((early_weight, early_dir)):
+            wait_bytes(buffer.at[way], early_recv.at[kind, way])
+        form_weights(ATTN, 1, owner, (FIRST, EARLY), early_weight.at[way], early_dir.at[way], None)
+
     def send_pair(place, chunk):
         send(place, place, sent.at[1, chunk], pair_recv.at[chunk], peer)
 
@@ -424,9 +448,11 @@
     for bank in (ATTN, MLP):
         wait_bytes(replicas[bank].at[:, pl.ds(0, LENGTHS[bank] // 2)], pair_recv.at[bank])
         wait_bytes(replicas[bank], sent.at[0, bank])
-        wait_bytes(replicas[bank].at[:, pl.ds(0, len(FAR_FIRST) * SHARDS[bank][1])], sent.at[1, bank])
+        columns = len(FAR_FIRST) * SHARDS[bank][1] - (EARLY if bank == ATTN else 0)
+        wait_bytes(replicas[bank].at[:, pl.ds(0, columns)], sent.at[1, bank])
     wait_bytes(all_small, sent.at[0, SMALL])
     wait_bytes(all_small.at[pl.ds(0, len(FAR_FIRST))], sent.at[1, SMALL])
+    wait_bytes(early_dir, early_sent.at[1])
     for which, tiles in enumerate((start_tiles, first_tiles, rest_tiles)):
         wait_bytes(tiles.at[pl.ds(0, len(FAR_FIRST))], tile_sent.at[which])
 
@@ -454,12 +480,12 @@
     scratch = [
         pltpu.VMEM((2, 2, 4, *attn), bf16), pltpu.VMEM((2, 2, 4, *mlp), bf16), pltpu.VMEM((2, 4, *small), bf16),
         *sums(2), pltpu.VMEM(small, f32), *sums(2), pltpu.VMEM(small, f32), *sums(2), pltpu.VMEM(small, f32), *sums(2),
-        pltpu.VMEM((VEC, LANES), bf16), pltpu.VMEM((TALL, BLOCK), bf16), pltpu.VMEM((8, *small), bf16),
+        *[pltpu.VMEM((2, FIRST, EARLY), f32)] * 2, pltpu.VMEM((VEC, LANES), bf16), pltpu.VMEM((TALL, BLOCK), bf16), pltpu.VMEM((8, *small), bf16),
         pltpu.VMEM((8, *small), bf16),
         pltpu.VMEM((VEC_PAD, LANES), f32), pltpu.VMEM((LANES, VEC_PAD), f32), pltpu.VMEM((8, VEC_PAD), f32),
         *[pltpu.VMEM((8, 8, LANES), f32)] * 3, pltpu.VMEM((LANES, LANES), f32),
         dma((10,)), dma((2, 3)), dma((3,)), dma((2, 2, 2)), dma((2,)), dma((2, 3)), dma((3,)), dma((2, 3, 2)), dma((2, 3)),
-        dma((3,)),
+        dma((3,)), dma((2,)), dma((2, 2)),
     ]
     count = len(shapes)
     anywhere = [pl.BlockSpec(memory_space=pl.ANY)] * count

time: 98.1 us -> 97.3 us (level)
  no operation moved by 1% of the time
where the time goes in v5:
time: 97.3 us; the launch traced here: 97.1 us
  Pallas kernels  96.5 us (99%)
    pallas_call x2, Pallas kernels, local_step(): results = finish(*step(*banks))  96.5 us

profile of v5, /device:TPU:0, one launch (start us, length us, event | category | flops | bytes accessed | tf_op | source)
XLA Modules:
  0.0 97.1 jit_solution(4231158677228692198)
XLA Ops:
  0.7 92.2 %lamb_step.1 = (bf16[64,16384]{1,0:T(8,128)(2,1)S(1)}, bf16[32,65536]{1,0:T(8,128)(2,1)S(1)}, bf16[16,512]{1,0:T(8,128)(2,1)S(1)}, bf16[146,128]{1,0:T(8,128)(2,...) custom-call(bf16[64,16384]{1,0:T(8,128)(2,1)} %bitcast.11, ...), custom_call_target="tpu_custom_call" | custom-call | tf_op jit(solution)/shard_map/lamb_step/pallas_call | solution.py:514
  92.9 4.2 %write_out.1 = (bf16[64,16384]{1,0:T(8,128)(2,1)}, bf16[32,65536]{1,0:T(8,128)(2,1)}, bf16[16,512]{1,0:T(8,128)(2,1)}, bf16[146,128]{1,0:T(8,128)(2,1)}, f32[64,...) custom-call(bf16[64,16384]{1,0:T(8,128)(2,1)S(1)} %get-tuple-element, ...), custom_call_target="tpu_custom_call" | custom-call | tf_op jit(solution)/shard_map/write_out/pallas_call | solution.py:514

commit v6 on v5

--- a/solution.py
+++ b/solution.py
@@ -27,11 +27,13 @@
 VEC_PAD = 256
 ATTN_SHARD = 2048
 MLP_SHARD = 8192
-STEP = 1024
-BLOCK = 512
+STEP = 2048
+BLOCK = 1024
+WIDE = 512
+TAIL = 640
 MIB = 2 ** 20
 ROWS = (HALF, 32, TALL, VEC)
-LENGTHS = (16384, 65536, BLOCK, LANES)
+LENGTHS = (16384, 65536, WIDE, LANES)
 SHARDS = ((HALF, ATTN_SHARD), (32, MLP_SHARD), (TALL, HALF), (TALL, VEC))
 ATTN, MLP, SMALL = range(3)
 BIG = (ATTN, MLP)
@@ -40,7 +42,7 @@
 PEER, ALONG_X, ALONG_Y = 1, 2, 4
 NEAR = ((ALONG_X, ALONG_Y), (ALONG_Y, ALONG_X))
 WIDE_LANES = (LANES, LANES + HALF)
-FAR_FIRST = tuple(reversed(range(1, 8)))
+FAR_FIRST = (6, 7, 4, 2, 5, 3, 1)
 
 
 def flip(index, mask):
@@ -88,7 +90,7 @@
      sum_attn, sum_mlp, sum_small, dir_attn, dir_mlp, early_weight, early_dir, vec_in, wide_in, small_out, all_small,
      vec_rows, vec_columns, vec_row, start_tiles, first_tiles, rest_tiles, row_acc,
      load_sems, sent, tile_sent, scatter_recv, small_recv, last_recv, tile_recv, own_recv, pass_recv, pair_recv,
-     early_sent, early_recv) = refs[32:]
+     early_sent, early_recv, tail_recv) = refs[32:]
     recvs, parts, lasts = (recv_attn, recv_mlp), (part_attn, part_mlp), (last_attn, last_mlp)
     me = lax.axis_index("data")
     core = me % 2
@@ -100,6 +102,11 @@
     def replica_chunk(half, owner, chunk):
         rows, columns = SHAPES[chunk]
         return replicas[chunk].at[pl.ds(rows * half, rows), aligned(owner, columns)]
+
+    def replica_part(half, owner, first, last):
+        rows, columns = SHAPES[ATTN]
+        start = pl.multiple_of(owner * columns + first, LANES)
+        return replicas[ATTN].at[pl.ds(rows * half, rows), pl.ds(start, last - first)]
 
     along_x, along_y = flip(me, ALONG_X), flip(me, ALONG_Y)
     small_near = (along_x * (1 - core) + along_y * core, along_y * (1 - core) + along_x * core)
@@ -354,7 +361,7 @@
     def send_own(half, chunk, way):
         place = all_small.at[me] if chunk == SMALL else replica_chunk(half, me, chunk)
         if (half, chunk) == (1, ATTN) and way:
-            place = replicas[ATTN].at[late_rows, pl.ds(pl.multiple_of(me * ATTN_SHARD + EARLY, BLOCK), ATTN_SHARD - EARLY)]
+            place = replica_part(1, me, EARLY, ATTN_SHARD)
         recv_sem = own_recv.at[half, chunk, way - 1] if way else pair_recv.at[chunk]
         own_copies[half, chunk, way] = send(place, place, sent.at[1, chunk], recv_sem, flip(me, (PEER, ALONG_X, ALONG_Y)[way]))
 
@@ -424,9 +431,16 @@
     for chunk in (MLP, ATTN):
         for half in HALVES:
             own_copies[half, chunk, 1 + half].wait_recv()
-            place = replica_chunk(half, flip(me, NEAR[half][0]), chunk)
-            passed[half, chunk] = send(place, place, sent.at[1, chunk], pass_recv.at[half, chunk], flip(me, NEAR[half][1]))
+            owner, target = flip(me, NEAR[half][0]), flip(me, NEAR[half][1])
+            place = replica_chunk(half, owner, chunk)
             send_pair(place, chunk)
+            if chunk == ATTN:
+                place = replica_part(half, owner, 0, ATTN_SHARD - TAIL)
+            passed[half, chunk] = send(place, place, sent.at[1, chunk], pass_recv.at[half, chunk], target)
+    for target_core in (0, 1):
+        for half in HALVES:
+            place = replica_part(half, flip(me, NEAR[half][0]), ATTN_SHARD - TAIL, ATTN_SHARD)
+            send(place, place, sent.at[1, ATTN], tail_recv, flip(me, NEAR[half][1] + (PEER if target_core else 0)))
     for chunk in BIG:
         for half in HALVES:
             own_copies[half, chunk, 2 - half].wait_recv()
@@ -441,20 +455,22 @@
         vec_columns[TALL * owner:TALL * owner + TALL, 0:VEC] = vecs[owner]
     vec_rows[...] = vec_columns[...].T
     replicas[3][...] = vec_rows[0:VEC, :].astype(jnp.bfloat16)
-    for chunk in (MLP, ATTN):
-        for half in HALVES:
-            passed[half, chunk].wait_recv()
-            send_pair(replica_chunk(half, far, chunk), chunk)
-    for bank in (ATTN, MLP):
-        wait_bytes(replicas[bank].at[:, pl.ds(0, LENGTHS[bank] // 2)], pair_recv.at[bank])
-        wait_bytes(replicas[bank], sent.at[0, bank])
-        columns = len(FAR_FIRST) * SHARDS[bank][1] - (EARLY if bank == ATTN else 0)
-        wait_bytes(replicas[bank].at[:, pl.ds(0, columns)], sent.at[1, bank])
     wait_bytes(all_small, sent.at[0, SMALL])
     wait_bytes(all_small.at[pl.ds(0, len(FAR_FIRST))], sent.at[1, SMALL])
     wait_bytes(early_dir, early_sent.at[1])
     for which, tiles in enumerate((start_tiles, first_tiles, rest_tiles)):
         wait_bytes(tiles.at[pl.ds(0, len(FAR_FIRST))], tile_sent.at[which])
+    for bank in BIG:
+        wait_bytes(replicas[bank], sent.at[0, bank])
+    for chunk in (MLP, ATTN):
+        for half in HALVES:
+            passed[half, chunk].wait_recv()
+            send_pair(replica_part(half, far, 0, ATTN_SHARD - TAIL) if chunk == ATTN else replica_chunk(half, far, chunk), chunk)
+    for bank, received, gone in ((MLP, 0, 0), (ATTN, TAIL, EARLY)):
+        columns = SHAPES[bank][1]
+        wait_bytes(replicas[bank].at[:, pl.ds(0, 4 * columns - received)], pair_recv.at[bank])
+        wait_bytes(replicas[bank].at[:, pl.ds(0, len(FAR_FIRST) * columns - gone)], sent.at[1, bank])
+    wait_bytes(replicas[ATTN].at[:, pl.ds(0, 2 * TAIL)], tail_recv)
 
 
 def write_out(*refs):
@@ -480,12 +496,12 @@
     scratch = [
         pltpu.VMEM((2, 2, 4, *attn), bf16), pltpu.VMEM((2, 2, 4, *mlp), bf16), pltpu.VMEM((2, 4, *small), bf16),
         *sums(2), pltpu.VMEM(small, f32), *sums(2), pltpu.VMEM(small, f32), *sums(2), pltpu.VMEM(small, f32), *sums(2),
-        *[pltpu.VMEM((2, FIRST, EARLY), f32)] * 2, pltpu.VMEM((VEC, LANES), bf16), pltpu.VMEM((TALL, BLOCK), bf16), pltpu.VMEM((8, *small), bf16),
+        *[pltpu.VMEM((2, FIRST, EARLY), f32)] * 2, pltpu.VMEM((VEC, LANES), bf16), pltpu.VMEM((TALL, WIDE), bf16), pltpu.VMEM((8, *small), bf16),
         pltpu.VMEM((8, *small), bf16),
         pltpu.VMEM((VEC_PAD, LANES), f32), pltpu.VMEM((LANES, VEC_PAD), f32), pltpu.VMEM((8, VEC_PAD), f32),
         *[pltpu.VMEM((8, 8, LANES), f32)] * 3, pltpu.VMEM((LANES, LANES), f32),
         dma((10,)), dma((2, 3)), dma((3,)), dma((2, 2, 2)), dma((2,)), dma((2, 3)), dma((3,)), dma((2, 3, 2)), dma((2, 3)),
-        dma((3,)), dma((2,)), dma((2, 2)),
+        dma((3,)), dma((2,)), dma((2, 2)), dma,
     ]
     count = len(shapes)
     anywhere = [pl.BlockSpec(memory_space=pl.ANY)] * count

time: 97.3 us -> 96.6 us (level)
  no operation moved by 1% of the time
where the time goes in v6:
time: 96.6 us; the launch traced here: 96.4 us
  Pallas kernels  95.8 us (99%)
    pallas_call x2, Pallas kernels, local_step(): results = finish(*step(*banks))  95.8 us

profile of v6, /device:TPU:0, one launch (start us, length us, event | category | flops | bytes accessed | tf_op | source)
XLA Modules:
  0.0 96.4 jit_solution(2923544471509993391)
XLA Ops:
  0.7 91.6 %lamb_step.1 = (bf16[64,16384]{1,0:T(8,128)(2,1)S(1)}, bf16[32,65536]{1,0:T(8,128)(2,1)S(1)}, bf16[16,512]{1,0:T(8,128)(2,1)S(1)}, bf16[146,128]{1,0:T(8,128)(2,...) custom-call(bf16[64,16384]{1,0:T(8,128)(2,1)} %bitcast.11, ...), custom_call_target="tpu_custom_call" | custom-call | tf_op jit(solution)/shard_map/lamb_step/pallas_call | solution.py:530
  92.2 4.2 %write_out.1 = (bf16[64,16384]{1,0:T(8,128)(2,1)}, bf16[32,65536]{1,0:T(8,128)(2,1)}, bf16[16,512]{1,0:T(8,128)(2,1)}, bf16[146,128]{1,0:T(8,128)(2,1)}, f32[64,...) custom-call(bf16[64,16384]{1,0:T(8,128)(2,1)S(1)} %get-tuple-element, ...), custom_call_target="tpu_custom_call" | custom-call | tf_op jit(solution)/shard_map/write_out/pallas_call | solution.py:530

commit v7 on v6

--- a/solution.py
+++ b/solution.py
@@ -90,7 +90,7 @@
      sum_attn, sum_mlp, sum_small, dir_attn, dir_mlp, early_weight, early_dir, vec_in, wide_in, small_out, all_small,
      vec_rows, vec_columns, vec_row, start_tiles, first_tiles, rest_tiles, row_acc,
      load_sems, sent, tile_sent, scatter_recv, small_recv, last_recv, tile_recv, own_recv, pass_recv, pair_recv,
-     early_sent, early_recv, tail_recv) = refs[32:]
+     early_sent, early_recv, tail_recv, ready) = refs[32:]
     recvs, parts, lasts = (recv_attn, recv_mlp), (part_attn, part_mlp), (last_attn, last_mlp)
     me = lax.axis_index("data")
     core = me % 2
@@ -123,9 +123,18 @@
         pltpu.make_async_copy(ref, ref, sem).wait()
 
     barrier = pltpu.get_barrier_semaphore()
-    near = (1, 2, 3, 4, 5)
-    for mask in near:
-        pl.semaphore_signal(barrier, inc=1, device_id=(flip(me, mask),), device_id_type=MESH)
+
+    def signal(semaphore, device):
+        pl.semaphore_signal(semaphore, inc=1, device_id=(device,), device_id_type=MESH)
+
+    signal(barrier, peer)
+
+    @pl.when(core == 1)
+    def _():
+        for mask in (ALONG_X, ALONG_Y):
+            for device in (flip(me, mask), flip(peer, mask)):
+                signal(barrier, device)
+
 
     small_loads = [pltpu.make_async_copy(grads[2], wide_in, load_sems.at[2]),
                    pltpu.make_async_copy(grads[3], vec_in, load_sems.at[3])]
@@ -144,18 +153,32 @@
             copy.start()
             if bank >= 2:
                 state_loads.append(copy)
-    pl.semaphore_wait(barrier, len(near))
-
-    def scatter(keep, chunk):
-        for slot in (1, 2, 0):
+    pl.semaphore_wait(barrier, 3)
+
+    def scatter(keep, chunk, slots):
+        for slot in slots:
             for half in HALVES:
                 target = peer if slot == 0 else flip(me, NEAR[half][0]) // 2 * 2 + slot - 1
                 owner = target if keep else flip(target, NEAR[half][1])
                 send(grad_chunk(half, owner, chunk), recvs[chunk].at[half, keep, 1 if slot == 0 else 2 + core],
                      sent.at[0, chunk], scatter_recv.at[half, keep, chunk], target)
 
-    scatter(0, MLP)
-    scatter(0, ATTN)
+    for chunk in (MLP, ATTN):
+        scatter(0, chunk, (2, 0))
+
+    @pl.when(core == 1)
+    def _():
+        signal(ready, along_x)
+        signal(ready, along_y)
+        pl.semaphore_wait(ready, 2)
+        signal(ready, peer)
+
+    @pl.when(core == 0)
+    def _():
+        pl.semaphore_wait(ready, 1)
+
+    for chunk in (MLP, ATTN):
+        scatter(0, chunk, (1,))
     for copy in small_loads:
         copy.wait()
     vec_rows[...] = jnp.zeros_like(vec_rows)
@@ -180,8 +203,8 @@
         targets = [(target, target if keep else flip(target, way), 2 + core) for target, way in places]
         for target, owner, slot in [*targets, (peer, peer if keep else peer_next, 1)]:
             send(small_out.at[owner], recv_small.at[keep, slot], sent.at[0, SMALL], small_recv.at[keep], target)
-    scatter(1, MLP)
-    scatter(1, ATTN)
+    for chunk in (MLP, ATTN):
+        scatter(1, chunk, (1, 2, 0))
 
     row = lax.broadcasted_iota(jnp.int32, (LANES, LANES), 0)
     lane = lax.broadcasted_iota(jnp.int32, (LANES, LANES), 1)
@@ -475,7 +498,8 @@
 
 def write_out(*refs):
     count = (len(refs) - 1) // 2
-    copies = [pltpu.make_async_copy(refs[k], refs[count + k], refs[-1]) for k in range(count)]
+    largest_first = sorted(range(count), key=lambda k: -refs[k].size)
+    copies = [pltpu.make_async_copy(refs[k], refs[count + k], refs[-1]) for k in largest_first]
     for copy in copies:
         copy.start()
     for copy in copies:
@@ -501,7 +525,7 @@
         pltpu.VMEM((VEC_PAD, LANES), f32), pltpu.VMEM((LANES, VEC_PAD), f32), pltpu.VMEM((8, VEC_PAD), f32),
         *[pltpu.VMEM((8, 8, LANES), f32)] * 3, pltpu.VMEM((LANES, LANES), f32),
         dma((10,)), dma((2, 3)), dma((3,)), dma((2, 2, 2)), dma((2,)), dma((2, 3)), dma((3,)), dma((2, 3, 2)), dma((2, 3)),
-        dma((3,)), dma((2,)), dma((2, 2)), dma,
+        dma((3,)), dma((2,)), dma((2, 2)), dma, pltpu.SemaphoreType.REGULAR,
     ]
     count = len(shapes)
     anywhere = [pl.BlockSpec(memory_space=pl.ANY)] * count

time: 96.6 us -> 95.9 us (level)
  no operation moved by 1% of the time
where the time goes in v7:
time: 95.9 us; the launch traced here: 95.8 us
  Pallas kernels  95.2 us (99%)
    pallas_call x2, Pallas kernels, local_step(): results = finish(*step(*banks))  95.2 us

profile of v7, /device:TPU:0, one launch (start us, length us, event | category | flops | bytes accessed | tf_op | source)
XLA Modules:
  0.0 95.8 jit_solution(16794539491513115724)
XLA Ops:
  0.7 91.1 %lamb_step.1 = (bf16[64,16384]{1,0:T(8,128)(2,1)S(1)}, bf16[32,65536]{1,0:T(8,128)(2,1)S(1)}, bf16[16,512]{1,0:T(8,128)(2,1)S(1)}, bf16[146,128]{1,0:T(8,128)(2,...) custom-call(bf16[64,16384]{1,0:T(8,128)(2,1)} %bitcast.11, ...), custom_call_target="tpu_custom_call" | custom-call | tf_op jit(solution)/shard_map/lamb_step/pallas_call | solution.py:554
  91.7 4.1 %write_out.1 = (bf16[64,16384]{1,0:T(8,128)(2,1)}, bf16[32,65536]{1,0:T(8,128)(2,1)}, bf16[16,512]{1,0:T(8,128)(2,1)}, bf16[146,128]{1,0:T(8,128)(2,1)}, f32[64,...) custom-call(bf16[64,16384]{1,0:T(8,128)(2,1)S(1)} %get-tuple-element, ...), custom_call_target="tpu_custom_call" | custom-call | tf_op jit(solution)/shard_map/write_out/pallas_call | solution.py:554

commit v8 on v7

--- a/solution.py
+++ b/solution.py
@@ -87,9 +87,9 @@
     grads, weights, firsts, seconds = refs[0:4], refs[4:8], refs[8:12], refs[12:16]
     replicas, new_weights, new_firsts, new_seconds = refs[16:20], refs[20:24], refs[24:28], refs[28:32]
     (recv_attn, recv_mlp, recv_small, part_attn, part_mlp, part_small, last_attn, last_mlp, last_small,
-     sum_attn, sum_mlp, sum_small, dir_attn, dir_mlp, early_weight, early_dir, vec_in, wide_in, small_out, all_small,
-     vec_rows, vec_columns, vec_row, start_tiles, first_tiles, rest_tiles, row_acc,
-     load_sems, sent, tile_sent, scatter_recv, small_recv, last_recv, tile_recv, own_recv, pass_recv, pair_recv,
+     sum_attn, sum_mlp, sum_small, dir_attn, dir_mlp, early, state_wide, state_vec, vec_in, wide_in, small_out, all_small,
+     vec_rows, vec_columns, vec_row, all_tiles, row_acc,
+     load_sems, sent, tile_sent, scatter_recv, small_recv, last_recv, tile_recv, own_recv, own_small, pass_recv, pair_recv,
      early_sent, early_recv, tail_recv, ready) = refs[32:]
     recvs, parts, lasts = (recv_attn, recv_mlp), (part_attn, part_mlp), (last_attn, last_mlp)
     me = lax.axis_index("data")
@@ -136,8 +136,8 @@
                 signal(barrier, device)
 
 
-    small_loads = [pltpu.make_async_copy(grads[2], wide_in, load_sems.at[2]),
-                   pltpu.make_async_copy(grads[3], vec_in, load_sems.at[3])]
+    small_loads = [pltpu.make_async_copy(grads[2], wide_in, load_sems.at[4]),
+                   pltpu.make_async_copy(grads[3], vec_in, load_sems.at[5])]
     for copy in small_loads:
         copy.start()
     for keep in range(2):
@@ -145,14 +145,10 @@
             for chunk in (MLP, ATTN):
                 owner = me if keep else flip(me, NEAR[half][1])
                 pltpu.make_async_copy(grad_chunk(half, owner, chunk), recvs[chunk].at[half, keep, 0],
-                                      scatter_recv.at[half, keep, chunk]).start()
-    state_loads = []
+                                      scatter_recv.at[keep, chunk]).start()
     for index, (source, target) in enumerate(((weights, new_weights), (firsts, new_firsts), (seconds, new_seconds))):
-        for bank in range(4):
-            copy = pltpu.make_async_copy(source[bank], target[bank], load_sems.at[bank if bank < 2 else 2 * index + bank + 2])
-            copy.start()
-            if bank >= 2:
-                state_loads.append(copy)
+        for bank, place in enumerate((target[0], target[1], state_wide.at[index], state_vec.at[index])):
+            pltpu.make_async_copy(source[bank], place, load_sems.at[bank]).start()
     pl.semaphore_wait(barrier, 3)
 
     def scatter(keep, chunk, slots):
@@ -161,7 +157,7 @@
                 target = peer if slot == 0 else flip(me, NEAR[half][0]) // 2 * 2 + slot - 1
                 owner = target if keep else flip(target, NEAR[half][1])
                 send(grad_chunk(half, owner, chunk), recvs[chunk].at[half, keep, 1 if slot == 0 else 2 + core],
-                     sent.at[0, chunk], scatter_recv.at[half, keep, chunk], target)
+                     sent.at[0, chunk], scatter_recv.at[keep, chunk], target)
 
     for chunk in (MLP, ATTN):
         scatter(0, chunk, (2, 0))
@@ -226,14 +222,15 @@
             tile = jnp.where(sub == index, value, tile)
         return tile
 
-    def exchange(tiles, which, value):
-        tiles[me] = value
+    def exchange(which, value):
+        all_tiles[which, me] = value
+        place = all_tiles.at[which, me]
         for mask in FAR_FIRST:
-            send(tiles.at[me], tiles.at[me], tile_sent.at[which], tile_recv.at[which], flip(me, mask))
-
-    def collect(tiles, which):
-        wait_bytes(tiles.at[pl.ds(0, len(FAR_FIRST))], tile_recv.at[which])
-        return add_all([tiles[index] for index in range(8)])
+            send(place, place, tile_sent, tile_recv.at[which], flip(me, mask))
+
+    def collect(which):
+        wait_bytes(all_tiles.at[which, pl.ds(0, len(FAR_FIRST))], tile_recv.at[which])
+        return add_all([all_tiles[which, index] for index in range(8)])
 
     def by_rows(first, groups, columns, step):
         def group(g, carry):
@@ -251,12 +248,12 @@
 
     for buffer, sem in ((recv_attn, load_sems.at[ATTN]), (recv_mlp, load_sems.at[MLP])):
         wait_bytes(buffer.at[:, :, pl.ds(0, 3)], sem)
-    for copy in state_loads:
-        copy.wait()
+    for bank, buffer in ((2, state_wide), (3, state_vec)):
+        wait_bytes(buffer, load_sems.at[bank])
     row_acc[...] = jnp.zeros_like(row_acc)
     by_rows(0, 8, ATTN_SHARD, square_of(new_weights[0]))
     by_rows(HALF, 4, MLP_SHARD, square_of(new_weights[1]))
-    wide_weight, vec_weight = new_weights[2][...], new_weights[3][...]
+    wide_weight, vec_weight = state_wide[0], state_vec[0]
     row_acc[96:112, 0:HALF] = wide_weight * wide_weight
     weight_lanes = lanes_of(0, LANES)
     weight_low, weight_high = vec_lanes(vec_weight * vec_weight)
@@ -268,44 +265,41 @@
                 lambda first, j, carry: step((pl.ds(first, TALL), aligned(j, BLOCK)), carry), r), init)
         return init
 
-    def gather_sum(half, keep, chunk):
-        source, target = recvs[chunk].at[half, keep], ((sum_attn, sum_mlp) if keep else parts)[chunk].at[half]
-        wait_bytes(source, scatter_recv.at[half, keep, chunk])
-
-        def step(place, carry):
-            value = [source[(slot, *place)].astype(jnp.float32) for slot in range(4)]
-            target[place] = (value[0] + value[1]) + (value[2] + value[3])
-            return carry
-
-        by_blocks(SHAPES[chunk], step, 0)
+    def gather_sum(keep, chunk):
+        wait_bytes(recvs[chunk].at[:, keep], scatter_recv.at[keep, chunk])
+        for half in HALVES:
+            source, target = recvs[chunk].at[half, keep], ((sum_attn, sum_mlp) if keep else parts)[chunk].at[half]
+
+            def step(place, carry):
+                value = [source[(slot, *place)].astype(jnp.float32) for slot in range(4)]
+                target[place] = (value[0] + value[1]) + (value[2] + value[3])
+                return carry
+
+            by_blocks(SHAPES[chunk], step, 0)
 
     def gather_small(keep, target):
         wait_bytes(recv_small.at[keep, pl.ds(1, 3)], small_recv.at[keep])
         target[...] = add_all([recv_small[keep, slot].astype(jnp.float32) for slot in range(4)])
 
-    last = {}
-    for chunk in (MLP, ATTN):
-        for half in HALVES:
-            gather_sum(half, 0, chunk)
+    for chunk in (MLP, ATTN):
+        gather_sum(0, chunk)
     gather_small(0, part_small)
-    last_small_copy = send(part_small, last_small, sent.at[0, SMALL], last_recv.at[0, SMALL], small_near[1])
-    for chunk in (MLP, ATTN):
-        for half in HALVES:
-            last[half, chunk] = send(parts[chunk].at[half], lasts[chunk].at[half], sent.at[0, chunk],
-                                     last_recv.at[half, chunk], flip(me, NEAR[half][1]))
-    for chunk in (MLP, ATTN):
-        for half in HALVES:
-            gather_sum(half, 1, chunk)
+    send(part_small, last_small, sent.at[0, SMALL], last_recv.at[SMALL], small_near[1])
+    for chunk in (MLP, ATTN):
+        for half in HALVES:
+            send(parts[chunk].at[half], lasts[chunk].at[half], sent.at[0, chunk], last_recv.at[chunk], flip(me, NEAR[half][1]))
+    for chunk in (MLP, ATTN):
+        gather_sum(1, chunk)
     gather_small(1, sum_small)
 
-    last_small_copy.wait_recv()
+    wait_bytes(last_small, last_recv.at[SMALL])
     wide_total, vec_total = small_parts(sum_small[...] + last_small[...])
     square = fold(jnp.concatenate([wide_total * wide_total, jnp.zeros((TALL, HALF), jnp.float32)], axis=1))
     low, high = vec_lanes(vec_total * vec_total)
     square = square + tile_of([low, high])
     for chunk in (MLP, ATTN):
-        for half in HALVES:
-            last[half, chunk].wait_recv()
+        wait_bytes(lasts[chunk], last_recv.at[chunk])
+        for half in HALVES:
             total, rest = (sum_attn, sum_mlp)[chunk].at[half], lasts[chunk].at[half]
 
             def step(place, acc):
@@ -315,16 +309,16 @@
 
             square = by_blocks(SHAPES[chunk], step, square)
 
-    exchange(start_tiles, 0, tile_of([weight_lanes, weight_low, weight_high, jnp.sum(square, axis=0, keepdims=True)]))
+    exchange(0, tile_of([weight_lanes, weight_low, weight_high, jnp.sum(square, axis=0, keepdims=True)]))
     late_rows = pl.ds(FIRST, FIRST)
     early_columns = pl.ds(0, EARLY)
 
-    def send_early(kind, source, buffer):
+    def send_early(kind, source):
         for way, mask in enumerate((ALONG_X, ALONG_Y)):
-            send(source, buffer.at[way], early_sent.at[kind], early_recv.at[kind, way], flip(me, mask))
-
-    send_early(0, new_weights[ATTN].at[late_rows, early_columns], early_weight)
-    start = collect(start_tiles, 0)
+            send(source, early.at[kind, way], early_sent.at[kind], early_recv, flip(me, mask))
+
+    send_early(0, new_weights[ATTN].at[late_rows, early_columns])
+    start = collect(0)
     square = jnp.sum(jnp.sum(start[3:4, :], axis=1, keepdims=True), axis=0, keepdims=True)
     clip = jnp.minimum(1.0, (8.0 * MAX_NORM) / jnp.sqrt(jnp.broadcast_to(square, (8, LANES)))) * 0.125
     clip_block = jnp.concatenate([clip] * (STEP // LANES), axis=1)
@@ -359,34 +353,36 @@
 
         by_blocks(SHAPES[bank], step, 0)
 
-    def update_small(bank, total, weight):
-        new_first, new_second = moments(new_firsts[bank][...], new_seconds[bank][...], total, clip[0:1, 0:1])
+    def update_small(bank, total, state):
+        new_first, new_second = moments(state[1], state[2], total, clip[0:1, 0:1])
         new_firsts[bank][...] = new_first
         new_seconds[bank][...] = new_second
-        return direction(new_first, new_second, weight)
+        return direction(new_first, new_second, state[0])
 
     update(ATTN, 0)
-    exchange(first_tiles, 1, tile_of([lanes_of(0, FIRST)]))
+    exchange(1, tile_of([lanes_of(0, FIRST)]))
     update(ATTN, 1)
-    send_early(1, dir_attn.at[1, :, early_columns], early_dir)
+    send_early(1, dir_attn.at[1, :, early_columns])
     for half in HALVES:
         update(MLP, half)
-    wide_dir = update_small(2, wide_total, wide_weight)
-    vec_dir = update_small(3, vec_total, vec_weight)
+    wide_dir = update_small(2, wide_total, state_wide)
+    vec_dir = update_small(3, vec_total, state_vec)
     row_acc[96:112, 0:HALF] = wide_dir * wide_dir
-    exchange(rest_tiles, 2, tile_of([lanes_of(FIRST, LANES), *vec_lanes(vec_dir * vec_dir)]))
+    exchange(2, tile_of([lanes_of(FIRST, LANES), *vec_lanes(vec_dir * vec_dir)]))
     for bank in (ATTN, MLP):
         for half in HALVES:
             store_moments(bank, half)
-
-    own_copies = {}
 
     def send_own(half, chunk, way):
         place = all_small.at[me] if chunk == SMALL else replica_chunk(half, me, chunk)
         if (half, chunk) == (1, ATTN) and way:
             place = replica_part(1, me, EARLY, ATTN_SHARD)
-        recv_sem = own_recv.at[half, chunk, way - 1] if way else pair_recv.at[chunk]
-        own_copies[half, chunk, way] = send(place, place, sent.at[1, chunk], recv_sem, flip(me, (PEER, ALONG_X, ALONG_Y)[way]))
+        recv_sem = pair_recv.at[chunk] if not way else own_small if chunk == SMALL else own_recv.at[(way - 1 + half) % 2, chunk]
+        send(place, place, sent.at[1, chunk], recv_sem, flip(me, (PEER, ALONG_X, ALONG_Y)[way]))
+
+    def wait_own(kind, chunk):
+        columns = SHAPES[chunk][1] - (EARLY // 2 if chunk == ATTN else 0)
+        wait_bytes(replicas[chunk].at[:, pl.ds(0, columns)], own_recv.at[kind, chunk])
 
     def spread_ratio(first, last, ratio):
         row_acc[first:last, :] = jnp.broadcast_to(
@@ -414,11 +410,11 @@
         for way in ways:
             send_own(half, bank, way)
 
-    spread_ratio(0, FIRST, weight_norms / jnp.sqrt(collect(first_tiles, 1)))
+    spread_ratio(0, FIRST, weight_norms / jnp.sqrt(collect(1)))
     new_weight(ATTN, 0, (1, 2, 0))
-    ratio = weight_norms / jnp.sqrt(collect(rest_tiles, 2))
+    ratio = weight_norms / jnp.sqrt(collect(2))
     spread_ratio(FIRST, LANES, ratio)
-    wait_bytes(early_weight, early_sent.at[0])
+    wait_bytes(early.at[0], early_sent.at[0])
     new_weight(ATTN, 1, (2, 0))
     for half in HALVES:
         new_weight(MLP, half, (1 + half, 0))
@@ -436,40 +432,37 @@
     for half in HALVES:
         send_own(half, MLP, 2 - half)
 
+    wait_bytes(early, early_recv)
     for way, owner in enumerate((along_x, along_y)):
-        for kind, buffer in enumerate((early_weight, early_dir)):
-            wait_bytes(buffer.at[way], early_recv.at[kind, way])
-        form_weights(ATTN, 1, owner, (FIRST, EARLY), early_weight.at[way], early_dir.at[way], None)
+        form_weights(ATTN, 1, owner, (FIRST, EARLY), early.at[0, way], early.at[1, way], None)
 
     def send_pair(place, chunk):
         send(place, place, sent.at[1, chunk], pair_recv.at[chunk], peer)
 
-    for way in (1, 2):
-        own_copies[0, SMALL, way].wait_recv()
+    wait_bytes(all_small.at[pl.ds(0, 2)], own_small)
     place = all_small.at[small_near[0]]
-    passed_small = send(place, place, sent.at[1, SMALL], pass_recv.at[0, SMALL], small_near[1])
+    send(place, place, sent.at[1, SMALL], pass_recv.at[SMALL], small_near[1])
     for owner in small_near:
         send_pair(all_small.at[owner], SMALL)
-    passed = {}
-    for chunk in (MLP, ATTN):
-        for half in HALVES:
-            own_copies[half, chunk, 1 + half].wait_recv()
+    for chunk in (MLP, ATTN):
+        wait_own(0, chunk)
+        for half in HALVES:
             owner, target = flip(me, NEAR[half][0]), flip(me, NEAR[half][1])
             place = replica_chunk(half, owner, chunk)
             send_pair(place, chunk)
             if chunk == ATTN:
                 place = replica_part(half, owner, 0, ATTN_SHARD - TAIL)
-            passed[half, chunk] = send(place, place, sent.at[1, chunk], pass_recv.at[half, chunk], target)
+            send(place, place, sent.at[1, chunk], pass_recv.at[chunk], target)
     for target_core in (0, 1):
         for half in HALVES:
             place = replica_part(half, flip(me, NEAR[half][0]), ATTN_SHARD - TAIL, ATTN_SHARD)
             send(place, place, sent.at[1, ATTN], tail_recv, flip(me, NEAR[half][1] + (PEER if target_core else 0)))
     for chunk in BIG:
-        for half in HALVES:
-            own_copies[half, chunk, 2 - half].wait_recv()
+        wait_own(1, chunk)
+        for half in HALVES:
             send_pair(replica_chunk(half, flip(me, NEAR[half][1]), chunk), chunk)
     far = flip(me, ALONG_X + ALONG_Y)
-    passed_small.wait_recv()
+    wait_bytes(all_small.at[pl.ds(0, 1)], pass_recv.at[SMALL])
     send_pair(all_small.at[far], SMALL)
     wait_bytes(all_small.at[pl.ds(0, 4)], pair_recv.at[SMALL])
     wides, vecs = zip(*(small_parts(all_small[owner].astype(jnp.float32)) for owner in range(8)))
@@ -480,14 +473,13 @@
     replicas[3][...] = vec_rows[0:VEC, :].astype(jnp.bfloat16)
     wait_bytes(all_small, sent.at[0, SMALL])
     wait_bytes(all_small.at[pl.ds(0, len(FAR_FIRST))], sent.at[1, SMALL])
-    wait_bytes(early_dir, early_sent.at[1])
-    for which, tiles in enumerate((start_tiles, first_tiles, rest_tiles)):
-        wait_bytes(tiles.at[pl.ds(0, len(FAR_FIRST))], tile_sent.at[which])
+    wait_bytes(early.at[1], early_sent.at[1])
+    wait_bytes(all_tiles.at[:, pl.ds(0, len(FAR_FIRST))], tile_sent)
     for bank in BIG:
         wait_bytes(replicas[bank], sent.at[0, bank])
-    for chunk in (MLP, ATTN):
-        for half in HALVES:
-            passed[half, chunk].wait_recv()
+    for chunk, gone in ((MLP, 0), (ATTN, TAIL)):
+        wait_bytes(replicas[chunk].at[:, pl.ds(0, SHAPES[chunk][1] - gone)], pass_recv.at[chunk])
+        for half in HALVES:
             send_pair(replica_part(half, far, 0, ATTN_SHARD - TAIL) if chunk == ATTN else replica_chunk(half, far, chunk), chunk)
     for bank, received, gone in ((MLP, 0, 0), (ATTN, TAIL, EARLY)):
         columns = SHAPES[bank][1]
@@ -520,12 +512,13 @@
     scratch = [
         pltpu.VMEM((2, 2, 4, *attn), bf16), pltpu.VMEM((2, 2, 4, *mlp), bf16), pltpu.VMEM((2, 4, *small), bf16),
         *sums(2), pltpu.VMEM(small, f32), *sums(2), pltpu.VMEM(small, f32), *sums(2), pltpu.VMEM(small, f32), *sums(2),
-        *[pltpu.VMEM((2, FIRST, EARLY), f32)] * 2, pltpu.VMEM((VEC, LANES), bf16), pltpu.VMEM((TALL, WIDE), bf16), pltpu.VMEM((8, *small), bf16),
+        pltpu.VMEM((2, 2, FIRST, EARLY), f32), pltpu.VMEM((3, *SHARDS[2]), f32), pltpu.VMEM((3, *SHARDS[3]), f32),
+        pltpu.VMEM((VEC, LANES), bf16), pltpu.VMEM((TALL, WIDE), bf16), pltpu.VMEM((8, *small), bf16),
         pltpu.VMEM((8, *small), bf16),
         pltpu.VMEM((VEC_PAD, LANES), f32), pltpu.VMEM((LANES, VEC_PAD), f32), pltpu.VMEM((8, VEC_PAD), f32),
-        *[pltpu.VMEM((8, 8, LANES), f32)] * 3, pltpu.VMEM((LANES, LANES), f32),
-        dma((10,)), dma((2, 3)), dma((3,)), dma((2, 2, 2)), dma((2,)), dma((2, 3)), dma((3,)), dma((2, 3, 2)), dma((2, 3)),
-        dma((3,)), dma((2,)), dma((2, 2)), dma, pltpu.SemaphoreType.REGULAR,
+        pltpu.VMEM((3, 8, 8, LANES), f32), pltpu.VMEM((LANES, LANES), f32),
+        dma((6,)), dma((2, 3)), dma, dma((2, 2)), dma((2,)), dma((3,)), dma((3,)), dma((2, 2)), dma, dma((3,)), dma((3,)),
+        dma((2,)), dma, dma, pltpu.SemaphoreType.REGULAR,
     ]
     count = len(shapes)
     anywhere = [pl.BlockSpec(memory_space=pl.ANY)] * count

time: 95.9 us -> 95.8 us (level)
  no operation moved by 1% of the time
where the time goes in v8:
time: 95.8 us; the launch traced here: 95.7 us
  Pallas kernels  95.1 us (99%)
    pallas_call x2, Pallas kernels, local_step(): results = finish(*step(*banks))  95.1 us

profile of v8, /device:TPU:0, one launch (start us, length us, event | category | flops | bytes accessed | tf_op | source)
XLA Modules:
  0.0 95.7 jit_solution(2502739639692410906)
XLA Ops:
  0.7 91.0 %lamb_step.1 = (bf16[64,16384]{1,0:T(8,128)(2,1)S(1)}, bf16[32,65536]{1,0:T(8,128)(2,1)S(1)}, bf16[16,512]{1,0:T(8,128)(2,1)S(1)}, bf16[146,128]{1,0:T(8,128)(2,...) custom-call(bf16[64,16384]{1,0:T(8,128)(2,1)} %bitcast.11, ...), custom_call_target="tpu_custom_call" | custom-call | tf_op jit(solution)/shard_map/lamb_step/pallas_call | solution.py:547
  91.6 4.1 %write_out.1 = (bf16[64,16384]{1,0:T(8,128)(2,1)}, bf16[32,65536]{1,0:T(8,128)(2,1)}, bf16[16,512]{1,0:T(8,128)(2,1)}, bf16[146,128]{1,0:T(8,128)(2,1)}, f32[64,...) custom-call(bf16[64,16384]{1,0:T(8,128)(2,1)S(1)} %get-tuple-element, ...), custom_call_target="tpu_custom_call" | custom-call | tf_op jit(solution)/shard_map/write_out/pallas_call | solution.py:547

commit v9 on v8

--- a/solution.py
+++ b/solution.py
@@ -31,6 +31,7 @@
 BLOCK = 1024
 WIDE = 512
 TAIL = 640
+PASSED = ((0, 1024), (1024, ATTN_SHARD - TAIL))
 MIB = 2 ** 20
 ROWS = (HALF, 32, TALL, VEC)
 LENGTHS = (16384, 65536, WIDE, LANES)
@@ -43,6 +44,7 @@
 NEAR = ((ALONG_X, ALONG_Y), (ALONG_Y, ALONG_X))
 WIDE_LANES = (LANES, LANES + HALF)
 FAR_FIRST = (6, 7, 4, 2, 5, 3, 1)
+TILE_ROWS = (4, 1, 3)
 
 
 def flip(index, mask):
@@ -90,7 +92,7 @@
      sum_attn, sum_mlp, sum_small, dir_attn, dir_mlp, early, state_wide, state_vec, vec_in, wide_in, small_out, all_small,
      vec_rows, vec_columns, vec_row, all_tiles, row_acc,
      load_sems, sent, tile_sent, scatter_recv, small_recv, last_recv, tile_recv, own_recv, own_small, pass_recv, pair_recv,
-     early_sent, early_recv, tail_recv, ready) = refs[32:]
+     early_sent, early_recv, tail_recv, attn_pass_recv, ready) = refs[32:]
     recvs, parts, lasts = (recv_attn, recv_mlp), (part_attn, part_mlp), (last_attn, last_mlp)
     me = lax.axis_index("data")
     core = me % 2
@@ -224,13 +226,14 @@
 
     def exchange(which, value):
         all_tiles[which, me] = value
-        place = all_tiles.at[which, me]
+        place = all_tiles.at[which, me, pl.ds(0, TILE_ROWS[which])]
         for mask in FAR_FIRST:
             send(place, place, tile_sent, tile_recv.at[which], flip(me, mask))
 
     def collect(which):
-        wait_bytes(all_tiles.at[which, pl.ds(0, len(FAR_FIRST))], tile_recv.at[which])
-        return add_all([all_tiles[which, index] for index in range(8)])
+        rows = TILE_ROWS[which]
+        wait_bytes(all_tiles.at[which, pl.ds(0, len(FAR_FIRST)), pl.ds(0, rows)], tile_recv.at[which])
+        return add_all([all_tiles[which, index, 0:rows] for index in range(8)])
 
     def by_rows(first, groups, columns, step):
         def group(g, carry):
@@ -241,7 +244,7 @@
                 0, columns // STEP, inner, jnp.zeros((8, LANES), jnp.float32))
             return carry
 
-        lax.fori_loop(0, groups, group, 0)
+        lax.fori_loop(0, groups, group, 0, unroll=4)
 
     def square_of(ref):
         return lambda place: fold(ref[place] * ref[place])
@@ -262,7 +265,7 @@
         rows, columns = shape
         for r in range(0, rows, TALL):
             init = lax.fori_loop(0, columns // BLOCK, functools.partial(
-                lambda first, j, carry: step((pl.ds(first, TALL), aligned(j, BLOCK)), carry), r), init)
+                lambda first, j, carry: step((pl.ds(first, TALL), aligned(j, BLOCK)), carry), r), init, unroll=2)
         return init
 
     def gather_sum(keep, chunk):
@@ -410,9 +413,9 @@
         for way in ways:
             send_own(half, bank, way)
 
-    spread_ratio(0, FIRST, weight_norms / jnp.sqrt(collect(1)))
+    spread_ratio(0, FIRST, weight_norms[0:1, :] / jnp.sqrt(collect(1)))
     new_weight(ATTN, 0, (1, 2, 0))
-    ratio = weight_norms / jnp.sqrt(collect(2))
+    ratio = weight_norms[0:3, :] / jnp.sqrt(collect(2))
     spread_ratio(FIRST, LANES, ratio)
     wait_bytes(early.at[0], early_sent.at[0])
     new_weight(ATTN, 1, (2, 0))
@@ -450,9 +453,12 @@
             owner, target = flip(me, NEAR[half][0]), flip(me, NEAR[half][1])
             place = replica_chunk(half, owner, chunk)
             send_pair(place, chunk)
-            if chunk == ATTN:
-                place = replica_part(half, owner, 0, ATTN_SHARD - TAIL)
-            send(place, place, sent.at[1, chunk], pass_recv.at[chunk], target)
+            if chunk == MLP:
+                send(place, place, sent.at[1, MLP], pass_recv.at[MLP], target)
+    for index, (first, last) in enumerate(PASSED):
+        for half in HALVES:
+            place = replica_part(half, flip(me, NEAR[half][0]), first, last)
+            send(place, place, sent.at[1, ATTN], attn_pass_recv.at[index], flip(me, NEAR[half][1]))
     for target_core in (0, 1):
         for half in HALVES:
             place = replica_part(half, flip(me, NEAR[half][0]), ATTN_SHARD - TAIL, ATTN_SHARD)
@@ -474,13 +480,16 @@
     wait_bytes(all_small, sent.at[0, SMALL])
     wait_bytes(all_small.at[pl.ds(0, len(FAR_FIRST))], sent.at[1, SMALL])
     wait_bytes(early.at[1], early_sent.at[1])
-    wait_bytes(all_tiles.at[:, pl.ds(0, len(FAR_FIRST))], tile_sent)
+    wait_bytes(all_tiles.at[0, pl.ds(0, len(FAR_FIRST))], tile_sent)
     for bank in BIG:
         wait_bytes(replicas[bank], sent.at[0, bank])
-    for chunk, gone in ((MLP, 0), (ATTN, TAIL)):
-        wait_bytes(replicas[chunk].at[:, pl.ds(0, SHAPES[chunk][1] - gone)], pass_recv.at[chunk])
-        for half in HALVES:
-            send_pair(replica_part(half, far, 0, ATTN_SHARD - TAIL) if chunk == ATTN else replica_chunk(half, far, chunk), chunk)
+    wait_bytes(replicas[MLP].at[:, pl.ds(0, MLP_SHARD)], pass_recv.at[MLP])
+    for half in HALVES:
+        send_pair(replica_chunk(half, far, MLP), MLP)
+    for index, (first, last) in enumerate(PASSED):
+        wait_bytes(replicas[ATTN].at[:, pl.ds(0, last - first)], attn_pass_recv.at[index])
+        for half in HALVES:
+            send_pair(replica_part(half, far, first, last), ATTN)
     for bank, received, gone in ((MLP, 0, 0), (ATTN, TAIL, EARLY)):
         columns = SHAPES[bank][1]
         wait_bytes(replicas[bank].at[:, pl.ds(0, 4 * columns - received)], pair_recv.at[bank])
@@ -518,7 +527,7 @@
         pltpu.VMEM((VEC_PAD, LANES), f32), pltpu.VMEM((LANES, VEC_PAD), f32), pltpu.VMEM((8, VEC_PAD), f32),
         pltpu.VMEM((3, 8, 8, LANES), f32), pltpu.VMEM((LANES, LANES), f32),
         dma((6,)), dma((2, 3)), dma, dma((2, 2)), dma((2,)), dma((3,)), dma((3,)), dma((2, 2)), dma, dma((3,)), dma((3,)),
-        dma((2,)), dma, dma, pltpu.SemaphoreType.REGULAR,
+        dma((2,)), dma, dma, dma((len(PASSED),)), pltpu.SemaphoreType.REGULAR,
     ]
     count = len(shapes)
     anywhere = [pl.BlockSpec(memory_space=pl.ANY)] * count

time: 95.8 us -> 95.2 us (level)
  no operation moved by 1% of the time
where the time goes in v9:
time: 95.2 us; the launch traced here: 95.1 us
  Pallas kernels  94.5 us (99%)
    pallas_call x2, Pallas kernels, local_step(): results = finish(*step(*banks))  94.5 us

profile of v9, /device:TPU:0, one launch (start us, length us, event | category | flops | bytes accessed | tf_op | source)
XLA Modules:
  0.0 95.1 jit_solution(76540465304206163)
XLA Ops:
  0.7 90.4 %lamb_step.1 = (bf16[64,16384]{1,0:T(8,128)(2,1)S(1)}, bf16[32,65536]{1,0:T(8,128)(2,1)S(1)}, bf16[16,512]{1,0:T(8,128)(2,1)S(1)}, bf16[146,128]{1,0:T(8,128)(2,...) custom-call(bf16[64,16384]{1,0:T(8,128)(2,1)} %bitcast.11, ...), custom_call_target="tpu_custom_call" | custom-call | tf_op jit(solution)/shard_map/lamb_step/pallas_call | solution.py:556
  91.0 4.1 %write_out.1 = (bf16[64,16384]{1,0:T(8,128)(2,1)}, bf16[32,65536]{1,0:T(8,128)(2,1)}, bf16[16,512]{1,0:T(8,128)(2,1)}, bf16[146,128]{1,0:T(8,128)(2,1)}, f32[64,...) custom-call(bf16[64,16384]{1,0:T(8,128)(2,1)S(1)} %get-tuple-element, ...), custom_call_target="tpu_custom_call" | custom-call | tf_op jit(solution)/shard_map/write_out/pallas_call | solution.py:556

commit v10 on v9

--- a/solution.py
+++ b/solution.py
@@ -16,6 +16,8 @@
 MAX_NORM = 1.0
 FIRST_SCALE = 1.0 / (1.0 - BETA_FIRST ** STEP_NUMBER)
 SECOND_SCALE = 1.0 / (1.0 - BETA_SECOND ** STEP_NUMBER)
+FIRST_FACTOR = FIRST_SCALE / SECOND_SCALE ** 0.5
+EPSILON_TERM = EPSILON / SECOND_SCALE ** 0.5
 
 MESH = pl.DeviceIdType.MESH
 LANES = 128
@@ -31,7 +33,7 @@
 BLOCK = 1024
 WIDE = 512
 TAIL = 640
-PASSED = ((0, 1024), (1024, ATTN_SHARD - TAIL))
+PASSED = ((0, 1152), (1152, ATTN_SHARD - TAIL))
 MIB = 2 ** 20
 ROWS = (HALF, 32, TALL, VEC)
 LENGTHS = (16384, 65536, WIDE, LANES)
@@ -43,7 +45,7 @@
 PEER, ALONG_X, ALONG_Y = 1, 2, 4
 NEAR = ((ALONG_X, ALONG_Y), (ALONG_Y, ALONG_X))
 WIDE_LANES = (LANES, LANES + HALF)
-FAR_FIRST = (6, 7, 4, 2, 5, 3, 1)
+FAR_FIRST = (6, 4, 2, 7, 5, 3, 1)
 TILE_ROWS = (4, 1, 3)
 
 
@@ -62,15 +64,14 @@
     return pl.ds(pl.multiple_of(index * size, size), size)
 
 
-def moments(first, second, total, clip):
-    clipped = clip * total
-    new_first = BETA_FIRST * first + (1.0 - BETA_FIRST) * clipped
-    new_second = BETA_SECOND * second + (1.0 - BETA_SECOND) * (clipped * clipped)
+def moments(first, second, total, factors):
+    new_first = BETA_FIRST * first + factors[0] * total
+    new_second = BETA_SECOND * second + factors[1] * (total * total)
     return new_first, new_second
 
 
 def direction(new_first, new_second, weight):
-    return (new_first * FIRST_SCALE) / (jnp.sqrt(new_second * SECOND_SCALE) + EPSILON) + WEIGHT_DECAY * weight
+    return (new_first * FIRST_FACTOR) / (jnp.sqrt(new_second) + EPSILON_TERM) + WEIGHT_DECAY * weight
 
 
 def fold(square):
@@ -324,7 +325,8 @@
     start = collect(0)
     square = jnp.sum(jnp.sum(start[3:4, :], axis=1, keepdims=True), axis=0, keepdims=True)
     clip = jnp.minimum(1.0, (8.0 * MAX_NORM) / jnp.sqrt(jnp.broadcast_to(square, (8, LANES)))) * 0.125
-    clip_block = jnp.concatenate([clip] * (STEP // LANES), axis=1)
+    factors = ((1.0 - BETA_FIRST) * clip, (1.0 - BETA_SECOND) * (clip * clip))
+    factor_blocks = [jnp.concatenate([factor] * (STEP // LANES), axis=1) for factor in factors]
     weight_norms = LEARN_RATE * jnp.sqrt(start)
 
     sums, directions = (sum_attn, sum_mlp), (dir_attn, dir_mlp)
@@ -335,7 +337,7 @@
         def step(place):
             state = (pl.ds(pl.multiple_of(half * rows + place[0].start, 8), 8), place[1])
             new_first, new_second = moments(
-                new_firsts[bank][state], new_seconds[bank][state], sums[bank].at[half][place], clip_block)
+                new_firsts[bank][state], new_seconds[bank][state], sums[bank].at[half][place], factor_blocks)
             value = direction(new_first, new_second, new_weights[bank][state])
             directions[bank].at[half][place] = value
             return fold(value * value)
@@ -347,9 +349,9 @@
 
         def step(place, carry):
             state = (pl.ds(half * rows + place[0].start, TALL), place[1])
-            clip_wide = jnp.concatenate([clip_block[:, 0:BLOCK]] * 2, axis=0)
+            wide_factors = [jnp.concatenate([block[:, 0:BLOCK]] * 2, axis=0) for block in factor_blocks]
             new_first, new_second = moments(
-                new_firsts[bank][state], new_seconds[bank][state], sums[bank].at[half][place], clip_wide)
+                new_firsts[bank][state], new_seconds[bank][state], sums[bank].at[half][place], wide_factors)
             new_firsts[bank][state] = new_first
             new_seconds[bank][state] = new_second
             return carry
@@ -357,7 +359,7 @@
         by_blocks(SHAPES[bank], step, 0)
 
     def update_small(bank, total, state):
-        new_first, new_second = moments(state[1], state[2], total, clip[0:1, 0:1])
+        new_first, new_second = moments(state[1], state[2], total, [factor[0:1, 0:1] for factor in factors])
         new_firsts[bank][...] = new_first
         new_seconds[bank][...] = new_second
         return direction(new_first, new_second, state[0])

time: 95.2 us -> 95 us (level)
  no operation moved by 1% of the time
where the time goes in v10:
time: 95 us; the launch traced here: 94.9 us
  Pallas kernels  94.3 us (99%)
    pallas_call x2, Pallas kernels, local_step(): results = finish(*step(*banks))  94.3 us

profile of v10, /device:TPU:0, one launch (start us, length us, event | category | flops | bytes accessed | tf_op | source)
XLA Modules:
  0.0 94.9 jit_solution(1391766826511278801)
XLA Ops:
  0.7 90.2 %lamb_step.1 = (bf16[64,16384]{1,0:T(8,128)(2,1)S(1)}, bf16[32,65536]{1,0:T(8,128)(2,1)S(1)}, bf16[16,512]{1,0:T(8,128)(2,1)S(1)}, bf16[146,128]{1,0:T(8,128)(2,...) custom-call(bf16[64,16384]{1,0:T(8,128)(2,1)} %bitcast.11, ...), custom_call_target="tpu_custom_call" | custom-call | tf_op jit(solution)/shard_map/lamb_step/pallas_call | solution.py:558
  90.8 4.1 %write_out.1 = (bf16[64,16384]{1,0:T(8,128)(2,1)}, bf16[32,65536]{1,0:T(8,128)(2,1)}, bf16[16,512]{1,0:T(8,128)(2,1)}, bf16[146,128]{1,0:T(8,128)(2,1)}, f32[64,...) custom-call(bf16[64,16384]{1,0:T(8,128)(2,1)S(1)} %get-tuple-element, ...), custom_call_target="tpu_custom_call" | custom-call | tf_op jit(solution)/shard_map/write_out/pallas_call | solution.py:558

commit v11 on v10

--- a/solution.py
+++ b/solution.py
@@ -289,9 +289,11 @@
         gather_sum(0, chunk)
     gather_small(0, part_small)
     send(part_small, last_small, sent.at[0, SMALL], last_recv.at[SMALL], small_near[1])
-    for chunk in (MLP, ATTN):
-        for half in HALVES:
-            send(parts[chunk].at[half], lasts[chunk].at[half], sent.at[0, chunk], last_recv.at[chunk], flip(me, NEAR[half][1]))
+    pieces = ((MLP, pl.ds(0, TALL), MLP), (ATTN, pl.ds(0, TALL), ATTN), (ATTN, pl.ds(TALL, TALL), 3))
+    for chunk, rows, index in pieces:
+        for half in HALVES:
+            send(parts[chunk].at[half, rows], lasts[chunk].at[half, rows], sent.at[0, chunk], last_recv.at[index],
+                 flip(me, NEAR[half][1]))
     for chunk in (MLP, ATTN):
         gather_sum(1, chunk)
     gather_small(1, sum_small)
@@ -301,17 +303,17 @@
     square = fold(jnp.concatenate([wide_total * wide_total, jnp.zeros((TALL, HALF), jnp.float32)], axis=1))
     low, high = vec_lanes(vec_total * vec_total)
     square = square + tile_of([low, high])
-    for chunk in (MLP, ATTN):
-        wait_bytes(lasts[chunk], last_recv.at[chunk])
-        for half in HALVES:
-            total, rest = (sum_attn, sum_mlp)[chunk].at[half], lasts[chunk].at[half]
+    for chunk, rows, index in pieces:
+        wait_bytes(lasts[chunk].at[:, rows], last_recv.at[index])
+        for half in HALVES:
+            total, rest = (sum_attn, sum_mlp)[chunk].at[half, rows], lasts[chunk].at[half, rows]
 
             def step(place, acc):
                 value = total[place] + rest[place]
                 total[place] = value
                 return acc + fold(value * value)
 
-            square = by_blocks(SHAPES[chunk], step, square)
+            square = by_blocks((TALL, SHAPES[chunk][1]), step, square)
 
     exchange(0, tile_of([weight_lanes, weight_low, weight_high, jnp.sum(square, axis=0, keepdims=True)]))
     late_rows = pl.ds(FIRST, FIRST)
@@ -528,7 +530,7 @@
         pltpu.VMEM((8, *small), bf16),
         pltpu.VMEM((VEC_PAD, LANES), f32), pltpu.VMEM((LANES, VEC_PAD), f32), pltpu.VMEM((8, VEC_PAD), f32),
         pltpu.VMEM((3, 8, 8, LANES), f32), pltpu.VMEM((LANES, LANES), f32),
-        dma((6,)), dma((2, 3)), dma, dma((2, 2)), dma((2,)), dma((3,)), dma((3,)), dma((2, 2)), dma, dma((3,)), dma((3,)),
+        dma((6,)), dma((2, 3)), dma, dma((2, 2)), dma((2,)), dma((4,)), dma((3,)), dma((2, 2)), dma, dma((3,)), dma((3,)),
         dma((2,)), dma, dma, dma((len(PASSED),)), pltpu.SemaphoreType.REGULAR,
     ]
     count = len(shapes)

time: 95 us -> 95 us (level)
  no operation moved by 1% of the time
where the time goes in v11:
time: 95 us; the launch traced here: 94.9 us
  Pallas kernels  94.3 us (99%)
    pallas_call x2, Pallas kernels, local_step(): results = finish(*step(*banks))  94.3 us

profile of v11, /device:TPU:0, one launch (start us, length us, event | category | flops | bytes accessed | tf_op | source)
XLA Modules:
  0.0 94.9 jit_solution(7393152935875522472)
XLA Ops:
  0.7 90.2 %lamb_step.1 = (bf16[64,16384]{1,0:T(8,128)(2,1)S(1)}, bf16[32,65536]{1,0:T(8,128)(2,1)S(1)}, bf16[16,512]{1,0:T(8,128)(2,1)S(1)}, bf16[146,128]{1,0:T(8,128)(2,...) custom-call(bf16[64,16384]{1,0:T(8,128)(2,1)} %bitcast.11, ...), custom_call_target="tpu_custom_call" | custom-call | tf_op jit(solution)/shard_map/lamb_step/pallas_call | solution.py:560
  90.8 4.1 %write_out.1 = (bf16[64,16384]{1,0:T(8,128)(2,1)}, bf16[32,65536]{1,0:T(8,128)(2,1)}, bf16[16,512]{1,0:T(8,128)(2,1)}, bf16[146,128]{1,0:T(8,128)(2,1)}, f32[64,...) custom-call(bf16[64,16384]{1,0:T(8,128)(2,1)S(1)} %get-tuple-element, ...), custom_call_target="tpu_custom_call" | custom-call | tf_op jit(solution)/shard_map/write_out/pallas_call | solution.py:560
